TPU v7x, 32 devices: a whole 2x2x4 slice. The times are simulated.
32 devices in a mesh: groups: 2 (over y), seq: 4 (over z), head: 2 (over x), sub: 2 (over core).
Axes of the slice: x: 2, y: 2, z: 4, core: 2. Of those that a mesh axis runs over, the one named last changes fastest.
Arguments:
- queries: bfloat16 [32, 64, 8192], P(('groups', 'seq'), None, 'head'), parts along dimension 0, may hold values from -6 to 6
- new_kv: bfloat16 [32, 64, 2, 1024], P(('groups', 'seq'), None, None, 'head'), parts along dimension 0, may hold values from -6 to 6
- kv_pages: bfloat16 [336, 2, 128, 1024], P(('groups', 'seq', 'sub'), None, None, 'head'), parts along dimension 0, may hold values from -6 to 6
- page_table: int32 [32, 16], P('groups'), parts along dimension 0, may hold values from -1 to 167, as said below
- cached_len: int32 [32], P('groups'), parts along dimension 0, may hold values from 1 to 2048, as said below
- is_prefill: int32 [32], P('groups'), parts along dimension 0, may hold values from 0 to 1, as said below
Outputs:
- attended: bfloat16 [32, 64, 8192], P(('groups', 'seq'), None, 'head'), parts along dimension 0
There are 2 independent parts, one for each index of `groups`. A program takes and returns all parts, laid end to end along the dimension named above; each array names one. Nothing has to cross between parts.
Inputs may be any that keep to these rules, and one draw needn't show every extreme that they name: `page_table`: entry [s, p] is the page number of page p of sequence s for p < ceil(cached_len[s] / 128) and -1 after; page number q lies on owner q // 21 (owner index = seq index * 2 + sub index) in its slot q % 21. Listing the pages of all sequences in order of sequence and page as t = 0, 1, ..., page t has owner (t + c) % 8 and slot (t + c) // 8 for one drawn c. No owner holds more than 8 page of the 4 sequences of one seq shard, and some owner holds exactly 8. `cached_len`: A decode sequence has 1 to 4 cache pages, a prefill sequence 8 to 16; all 4 sequences of one drawn seq shard are prefill sequences with 16 pages. `is_prefill`: exactly 8 sequences are prefill sequences.
All inputs are finite; a program needn't handle non-finite values.
Results may differ from a plain program's by a relative error of at most 0.014.
Values may be sent and summed in bfloat16 or wider, within the bound.
A program may use at most 64 MiB of HBM per device.

v0:
```python
import jax
import jax.numpy as jnp
from jax import lax
from jax.sharding import PartitionSpec as P

HD = 128
PAGE = 128


NEG_FILL = -1e30


def partial_softmax(
    query_heads, cache_keys, cache_values, cache_valid, fresh_keys, fresh_values, fresh_valid
):
    score_scale = HD ** (-0.5)
    cache_scores = (
        jnp.einsum("rkgd,nkd->kgrn", query_heads, cache_keys, preferred_element_type=jnp.float32)
        * score_scale
    )
    fresh_scores = (
        jnp.einsum("rkgd,jkd->kgrj", query_heads, fresh_keys, preferred_element_type=jnp.float32)
        * score_scale
    )
    cache_mask = cache_valid[None, None, None, :]
    fresh_mask = fresh_valid[None, None, :, :]
    peak = jnp.maximum(
        jnp.max(jnp.where(cache_mask, cache_scores, NEG_FILL), axis=-1),
        jnp.max(jnp.where(fresh_mask, fresh_scores, NEG_FILL), axis=-1),
    )
    cache_weights = jnp.where(cache_mask, jnp.exp(cache_scores - peak[..., None]), 0.0)
    fresh_weights = jnp.where(fresh_mask, jnp.exp(fresh_scores - peak[..., None]), 0.0)
    weight_sum = jnp.sum(cache_weights, axis=-1) + jnp.sum(fresh_weights, axis=-1)
    numerator = jnp.einsum(
        "kgrn,nkd->kgrd",
        cache_weights.astype(jnp.bfloat16),
        cache_values,
        preferred_element_type=jnp.float32,
    )
    numerator = numerator + jnp.einsum(
        "kgrj,jkd->kgrd",
        fresh_weights.astype(jnp.bfloat16),
        fresh_values,
        preferred_element_type=jnp.float32,
    )
    return (peak, weight_sum, numerator)


def attend_all(
    query_block, fresh_block, received, fetch_index, page_here, lengths, live_rows, causal, fresh_on
):
    kv_width = received.shape[-1]
    heads_kv = kv_width // HD
    row_count = query_block.shape[1]
    group_size = query_block.shape[2] // kv_width
    page_count = fetch_index.shape[1]
    positions = jnp.arange(page_count * PAGE, dtype=jnp.int32)

    def one_sequence(inputs):
        query_rows, fresh_rows, index_row, here_row, length, live_row = inputs
        fetched = jnp.take(received, index_row, axis=0)
        cache_keys = fetched[:, 0].reshape(page_count * PAGE, heads_kv, HD)
        cache_values = fetched[:, 1].reshape(page_count * PAGE, heads_kv, HD)
        page_mask = jnp.broadcast_to(here_row[:, None], (page_count, PAGE)).reshape(
            page_count * PAGE
        )
        cache_valid = page_mask & (positions < length)
        query_heads = query_rows.reshape(row_count, heads_kv, group_size, HD)
        fresh_keys = fresh_rows[:, 0].reshape(row_count, heads_kv, HD)
        fresh_values = fresh_rows[:, 1].reshape(row_count, heads_kv, HD)
        fresh_valid = causal & live_row[:, None] & fresh_on
        return partial_softmax(
            query_heads,
            cache_keys,
            cache_values,
            cache_valid,
            fresh_keys,
            fresh_values,
            fresh_valid,
        )

    return lax.map(
        one_sequence, (query_block, fresh_block, fetch_index, page_here, lengths, live_rows)
    )


def finish(weight_sum, numerator, live_rows):
    unused_rows = 1.0 - live_rows.astype(jnp.float32)
    attended = numerator / (weight_sum + unused_rows[:, None, None, :])[..., None]
    attended = jnp.where(live_rows[:, None, None, :, None], attended, 0.0)
    seq_dev, heads_kv, group_size, row_count, head_dim = attended.shape
    return (
        jnp.transpose(attended, (0, 3, 1, 2, 4))
        .reshape(seq_dev, row_count, heads_kv * group_size * head_dim)
        .astype(jnp.bfloat16)
    )


def per_device(queries, new_kv, kv_pages, page_table, cached_len, is_prefill):
    seq_shards = lax.axis_size("seq")
    sub_count = lax.axis_size("sub")
    owners = seq_shards * sub_count
    seq_index = lax.axis_index("seq")
    core_index = lax.axis_index("sub")
    owner_self = seq_index * sub_count + core_index
    seq_dev, row_count, query_width = queries.shape
    pages_dev = kv_pages.shape[0]
    kv_width = kv_pages.shape[3]
    page_count = page_table.shape[1]
    entries = seq_dev * page_count
    capacity = (entries + owners - 1) // owners
    table_rows = page_table.reshape(seq_shards, entries)
    holder = jnp.where(table_rows >= 0, table_rows // pages_dev, -1)
    slot_of = jnp.where(table_rows >= 0, table_rows % pages_dev, 0)
    owned_here = holder == owner_self
    rank_among = jnp.cumsum(owned_here.astype(jnp.int32), axis=1) - 1
    picked = owned_here[:, :, None] & (
        rank_among[:, :, None] == jnp.arange(capacity, dtype=jnp.int32)[None, None, :]
    )
    send_slots = jnp.sum(jnp.where(picked, slot_of[:, :, None], 0), axis=1).reshape(
        seq_shards * capacity
    )
    first_seq = seq_index * seq_dev
    my_table = lax.dynamic_slice_in_dim(page_table, first_seq, seq_dev, 0)
    my_lengths = lax.dynamic_slice_in_dim(cached_len, first_seq, seq_dev, 0)
    my_flags = lax.dynamic_slice_in_dim(is_prefill, first_seq, seq_dev, 0)
    flat_table = my_table.reshape(entries)
    my_holder = jnp.where(flat_table >= 0, flat_table // pages_dev, -1)
    entry_order = jnp.arange(entries, dtype=jnp.int32)
    earlier = (my_holder[:, None] == my_holder[None, :]) & (
        entry_order[None, :] < entry_order[:, None]
    )
    my_rank = jnp.sum(earlier.astype(jnp.int32), axis=1)
    row_ids = jnp.arange(row_count, dtype=jnp.int32)
    live_rows = (my_flags[:, None] == 1) | (row_ids[None, :] == 0)
    causal = row_ids[None, :] <= row_ids[:, None]
    part_width = kv_width // sub_count
    split_pages = kv_pages.reshape(pages_dev, 2, PAGE, sub_count, part_width)
    chosen = jnp.take(split_pages, send_slots, axis=0).reshape(
        seq_shards, capacity, 2, PAGE, sub_count, part_width
    )
    outgoing = jnp.moveaxis(chosen, 4, 1).reshape(owners, capacity, 2, PAGE, part_width)
    received = lax.all_to_all(
        outgoing, ("seq", "sub"), split_axis=0, concat_axis=0, tiled=True
    ).reshape(owners * capacity, 2, PAGE, part_width)
    present = flat_table >= 0
    fetch_index = jnp.where(present, my_holder * capacity + my_rank, 0)
    query_part = query_width // sub_count
    my_queries = lax.dynamic_slice_in_dim(queries, core_index * query_part, query_part, 2)
    my_fresh = lax.dynamic_slice_in_dim(new_kv, core_index * part_width, part_width, 3)
    peak, weight_sum, numerator = attend_all(
        my_queries,
        my_fresh,
        received,
        fetch_index.reshape(seq_dev, page_count),
        present.reshape(seq_dev, page_count),
        my_lengths,
        live_rows,
        causal,
        core_index >= 0,
    )
    own_heads = finish(weight_sum, numerator, live_rows)
    return lax.all_gather(own_heads, "sub", axis=2, tiled=True)


def solution(mesh):
    placed = (
        P(("groups", "seq"), None, "head"),
        P(("groups", "seq"), None, None, "head"),
        P(("groups", "seq", "sub"), None, None, "head"),
        P("groups", None),
        P("groups"),
        P("groups"),
    )
    return jax.shard_map(
        per_device,
        mesh=mesh,
        in_specs=placed,
        out_specs=P(("groups", "seq"), None, "head"),
        check_vma=False,
    )
```

profile of v0, /device:TPU:0, one launch (start us, length us, event | category | flops | bytes accessed | tf_op | source)
XLA Modules:
  0.0 370.2 jit_solution(17312206333277453594)
XLA Ops:
  8.9 12.1 %reshape.330 = bf16[21,2,128,2,256]{4,3,2,1,0:T(2,128)(2,1)} reshape(bf16[21,2,128,512]{3,2,1,0:T(8,128)(2,1)} %param.10) | data formatting | bytes 11010048 | tf_op jit(solution)/shard_map/reshape | solution.py:138
  21.1 20.8 %gather_fusion.1 = bf16[32,2,128,2,256]{4,3,2,1,0:T(2,128)(2,1)} fusion(bf16[21,2,128,2,256]{4,3,2,1,0:T(2,128)(2,1)} %reshape.330, s32[1024]{0:T(1024)S(1)} %pad_clamp_fusion.1), kind=kCustom, calls=%fused_computation.1 | custom fusion | bytes 16777344 | tf_op jit(solution)/shard_map/jit(_take)/gather | solution.py:139
  41.9 8.0 %copy_select_fusion = bf16[4,8,2,128,2,256]{5,3,2,1,4,0:T(8,128)(2,1)} fusion(bf16[4,8,2,128,2,256]{5,4,3,2,1,0:T(2,128)(2,1)} %bitcast.128, pred[4,8]{1,0:T(4,128)(4,1)S(1)} %compare_and_fusion.1), kind=kLoop, calls=%fused_computation.53 | loop fusion | flops 4194304 | bytes 16777248 | tf_op jit(solution)/shard_map/jit(_take)/select_n | solution.py:139
  49.9 6.5 %all-to-all-start = ((bf16[8,8,2,128,256]{4,3,2,1,0:T(8,128)(2,1)}), bf16[8,8,2,128,256]{4,3,2,1,0:T(8,128)(2,1)}, u32[]{:S(2)}, u32[]{:S(2)}) async-start(bf16[8,8,2,128,256]{4,3,2,1,0:T(8,128)(2,1)} %bitcast.129), calls=%async_computation | async-start | bytes 16777216 | tf_op jit(solution)/shard_map/all_to_all | solution.py:143
  58.4 1.1 constant_dynamic-slice_fusion.3
  59.5 180.9 %all-to-all-done = bf16[8,8,2,128,256]{4,3,2,1,0:T(8,128)(2,1)} async-done(((bf16[8,8,2,128,256]{4,3,2,1,0:T(8,128)(2,1)}), bf16[8,8,2,128,256]{4,3,2,1,0:T(8,128)(2,1)}, u32[]{:S(2)}, u32[]{:S(2)}) %all-to-all-start) | async-done | bytes 8388640 | tf_op jit(solution)/shard_map/all_to_all | solution.py:143
  240.3 106.1 %while.14 = (s32[]{:T(128)}, f32[4,2,8,64]{3,2,1,0:T(8,128)S(1)}, f32[4,2,8,64,128]{4,3,2,1,0:T(8,128)}, pred[4,16]{1,0:T(4,128)(4,1)S(1)}, s32[4]{0:T(128)S(1)}...) while((s32[]{:T(128)}, f32[4,2,8,64]{3,2,1,0:T(8,128)S(1)}, ...), condition=%wide.region_8.9_spmd.clone.clone, body=%wide.region_3.8_spmd.clone.sunk.clone | while | flops 1132149888 | bytes 48661236 | solution.py:82
  242.6 5.4 %gather_fusion = bf16[16,2,128,256]{3,2,1,0:T(8,128)(2,1)} fusion(bf16[64,2,128,256]{3,2,1,0:T(8,128)(2,1)} %get-tuple-element.285, s32[1024]{0:T(1024)S(1)} %pad_clamp_fusion.4), kind=kCustom, calls=%fused_computation.clone.clone.1.clone | custom fusion | bytes 4194368 | tf_op jit(solution)/shard_map/while/body/eval_jaxpr/jit(_take)/gather | solution.py:61
  248.1 1.9 broadcast_select_fusion.3
  250.4 4.7 %fusion.87 = (f32[2,8,64]{2,1,0:T(8,128)S(1)}, f32[2,2048,64,8]{1,2,3,0:T(8,128)}) fusion(pred[2048]{0:T(1024)(128)(4,1)S(1)} %fusion.84, bf16[64,2,8,128]{3,2,1,0:T(8,128)(2,1)S(1)} %bitcast.126, bf16[2048,2,128,1]{2,1,0,3:T(2,128)(2,1)S(1)} %bitcast.125), kind=kOutput, calls=%fused_computation.6.clone.1.clone | convolution fusion | flops 543161344 | bytes 9705472 | tf_op jit(solution)/shard_map/while/body/eval_jaxpr/rkgd,nkd->kgrn/dot_general | solution.py:18
  256.5 4.5 %fusion.90 = f32[2,8,64]{2,1,0:T(8,128)S(1)} fusion(f32[2,2048,64,8]{1,2,3,0:T(8,128)} %get-tuple-element.238, f32[2,8,64]{2,1,0:T(8,128)S(1)} %max.10, pred[2048]{0:T(1024)(128)(4,1)S(1)} %fusion.84), kind=kLoop, calls=%fused_computation.10.clone.1.clone | loop fusion | flops 8387584 | bytes 8398848 | tf_op jit(solution)/shard_map/while/body/eval_jaxpr/reduce_sum | solution.py:33
  261.4 4.4 %fusion.92 = f32[2,8,64,128]{3,2,1,0:T(8,128)S(1)} fusion(f32[2,2048,64,8]{1,2,3,0:T(8,128)} %get-tuple-element.238, f32[2,8,64]{2,1,0:T(8,128)S(1)} %max.10, pred[2048]{0:T(1024)(128)(4,1)S(1)} %fusion.84, bf16[2048,2,128,1]{2,1,0,3:T(2,128)(2,1)S(1)} %bitcast.130), kind=kOutput, calls=%fused_computation.11.clone.1.clone | convolution fusion | flops 545259520 | bytes 9967616 | tf_op jit(solution)/shard_map/while/body/eval_jaxpr/kgrn,nkd->kgrd/dot_general | solution.py:34
  265.8 1.1 fusion.93
  269.2 5.4 %gather_fusion = bf16[16,2,128,256]{3,2,1,0:T(8,128)(2,1)} fusion(bf16[64,2,128,256]{3,2,1,0:T(8,128)(2,1)} %get-tuple-element.285, s32[1024]{0:T(1024)S(1)} %pad_clamp_fusion.4), kind=kCustom, calls=%fused_computation.clone.clone.1.clone | custom fusion | bytes 4194368 | tf_op jit(solution)/shard_map/while/body/eval_jaxpr/jit(_take)/gather | solution.py:61
  274.6 1.9 broadcast_select_fusion.3
  276.9 4.7 %fusion.87 = (f32[2,8,64]{2,1,0:T(8,128)S(1)}, f32[2,2048,64,8]{1,2,3,0:T(8,128)}) fusion(pred[2048]{0:T(1024)(128)(4,1)S(1)} %fusion.84, bf16[64,2,8,128]{3,2,1,0:T(8,128)(2,1)S(1)} %bitcast.126, bf16[2048,2,128,1]{2,1,0,3:T(2,128)(2,1)S(1)} %bitcast.125), kind=kOutput, calls=%fused_computation.6.clone.1.clone | convolution fusion | flops 543161344 | bytes 9705472 | tf_op jit(solution)/shard_map/while/body/eval_jaxpr/rkgd,nkd->kgrn/dot_general | solution.py:18
  283.0 4.5 %fusion.90 = f32[2,8,64]{2,1,0:T(8,128)S(1)} fusion(f32[2,2048,64,8]{1,2,3,0:T(8,128)} %get-tuple-element.238, f32[2,8,64]{2,1,0:T(8,128)S(1)} %max.10, pred[2048]{0:T(1024)(128)(4,1)S(1)} %fusion.84), kind=kLoop, calls=%fused_computation.10.clone.1.clone | loop fusion | flops 8387584 | bytes 8398848 | tf_op jit(solution)/shard_map/while/body/eval_jaxpr/reduce_sum | solution.py:33
  287.9 4.4 %fusion.92 = f32[2,8,64,128]{3,2,1,0:T(8,128)S(1)} fusion(f32[2,2048,64,8]{1,2,3,0:T(8,128)} %get-tuple-element.238, f32[2,8,64]{2,1,0:T(8,128)S(1)} %max.10, pred[2048]{0:T(1024)(128)(4,1)S(1)} %fusion.84, bf16[2048,2,128,1]{2,1,0,3:T(2,128)(2,1)S(1)} %bitcast.130), kind=kOutput, calls=%fused_computation.11.clone.1.clone | convolution fusion | flops 545259520 | bytes 9967616 | tf_op jit(solution)/shard_map/while/body/eval_jaxpr/kgrn,nkd->kgrd/dot_general | solution.py:34
  295.7 5.4 %gather_fusion = bf16[16,2,128,256]{3,2,1,0:T(8,128)(2,1)} fusion(bf16[64,2,128,256]{3,2,1,0:T(8,128)(2,1)} %get-tuple-element.285, s32[1024]{0:T(1024)S(1)} %pad_clamp_fusion.4), kind=kCustom, calls=%fused_computation.clone.clone.1.clone | custom fusion | bytes 4194368 | tf_op jit(solution)/shard_map/while/body/eval_jaxpr/jit(_take)/gather | solution.py:61
  301.1 1.9 broadcast_select_fusion.3
  303.4 4.7 %fusion.87 = (f32[2,8,64]{2,1,0:T(8,128)S(1)}, f32[2,2048,64,8]{1,2,3,0:T(8,128)}) fusion(pred[2048]{0:T(1024)(128)(4,1)S(1)} %fusion.84, bf16[64,2,8,128]{3,2,1,0:T(8,128)(2,1)S(1)} %bitcast.126, bf16[2048,2,128,1]{2,1,0,3:T(2,128)(2,1)S(1)} %bitcast.125), kind=kOutput, calls=%fused_computation.6.clone.1.clone | convolution fusion | flops 543161344 | bytes 9705472 | tf_op jit(solution)/shard_map/while/body/eval_jaxpr/rkgd,nkd->kgrn/dot_general | solution.py:18
  309.5 4.5 %fusion.90 = f32[2,8,64]{2,1,0:T(8,128)S(1)} fusion(f32[2,2048,64,8]{1,2,3,0:T(8,128)} %get-tuple-element.238, f32[2,8,64]{2,1,0:T(8,128)S(1)} %max.10, pred[2048]{0:T(1024)(128)(4,1)S(1)} %fusion.84), kind=kLoop, calls=%fused_computation.10.clone.1.clone | loop fusion | flops 8387584 | bytes 8398848 | tf_op jit(solution)/shard_map/while/body/eval_jaxpr/reduce_sum | solution.py:33
  314.4 4.4 %fusion.92 = f32[2,8,64,128]{3,2,1,0:T(8,128)S(1)} fusion(f32[2,2048,64,8]{1,2,3,0:T(8,128)} %get-tuple-element.238, f32[2,8,64]{2,1,0:T(8,128)S(1)} %max.10, pred[2048]{0:T(1024)(128)(4,1)S(1)} %fusion.84, bf16[2048,2,128,1]{2,1,0,3:T(2,128)(2,1)S(1)} %bitcast.130), kind=kOutput, calls=%fused_computation.11.clone.1.clone | convolution fusion | flops 545259520 | bytes 9967616 | tf_op jit(solution)/shard_map/while/body/eval_jaxpr/kgrn,nkd->kgrd/dot_general | solution.py:34
  322.2 5.4 %gather_fusion = bf16[16,2,128,256]{3,2,1,0:T(8,128)(2,1)} fusion(bf16[64,2,128,256]{3,2,1,0:T(8,128)(2,1)} %get-tuple-element.285, s32[1024]{0:T(1024)S(1)} %pad_clamp_fusion.4), kind=kCustom, calls=%fused_computation.clone.clone.1.clone | custom fusion | bytes 4194368 | tf_op jit(solution)/shard_map/while/body/eval_jaxpr/jit(_take)/gather | solution.py:61
  327.6 1.9 broadcast_select_fusion.3
  329.9 4.7 %fusion.87 = (f32[2,8,64]{2,1,0:T(8,128)S(1)}, f32[2,2048,64,8]{1,2,3,0:T(8,128)}) fusion(pred[2048]{0:T(1024)(128)(4,1)S(1)} %fusion.84, bf16[64,2,8,128]{3,2,1,0:T(8,128)(2,1)S(1)} %bitcast.126, bf16[2048,2,128,1]{2,1,0,3:T(2,128)(2,1)S(1)} %bitcast.125), kind=kOutput, calls=%fused_computation.6.clone.1.clone | convolution fusion | flops 543161344 | bytes 9705472 | tf_op jit(solution)/shard_map/while/body/eval_jaxpr/rkgd,nkd->kgrn/dot_general | solution.py:18
  336.0 4.5 %fusion.90 = f32[2,8,64]{2,1,0:T(8,128)S(1)} fusion(f32[2,2048,64,8]{1,2,3,0:T(8,128)} %get-tuple-element.238, f32[2,8,64]{2,1,0:T(8,128)S(1)} %max.10, pred[2048]{0:T(1024)(128)(4,1)S(1)} %fusion.84), kind=kLoop, calls=%fused_computation.10.clone.1.clone | loop fusion | flops 8387584 | bytes 8398848 | tf_op jit(solution)/shard_map/while/body/eval_jaxpr/reduce_sum | solution.py:33
  340.9 4.4 %fusion.92 = f32[2,8,64,128]{3,2,1,0:T(8,128)S(1)} fusion(f32[2,2048,64,8]{1,2,3,0:T(8,128)} %get-tuple-element.238, f32[2,8,64]{2,1,0:T(8,128)S(1)} %max.10, pred[2048]{0:T(1024)(128)(4,1)S(1)} %fusion.84, bf16[2048,2,128,1]{2,1,0,3:T(2,128)(2,1)S(1)} %bitcast.130), kind=kOutput, calls=%fused_computation.11.clone.1.clone | convolution fusion | flops 545259520 | bytes 9967616 | tf_op jit(solution)/shard_map/while/body/eval_jaxpr/kgrn,nkd->kgrd/dot_general | solution.py:34
  346.4 2.1 fusion.35
  349.3 1.3 convert_element_type.37
  350.5 9.7 %all-gather.2.cloned.1.call-done = bf16[4,64,4096]{2,1,0:T(8,128)(2,1)} async-done(((bf16[4,64,2048]{2,1,0:T(8,128)(2,1)}), bf16[4,64,4096]{2,1,0:T(8,128)(2,1)}) %all-gather.2.cloned.1.call-update) | async-done | bytes 2097168 | tf_op jit(solution)/shard_map/all_gather | solution.py:163
  360.3 3.1 copy.115
  (137 shorter events, 26.3 us)
Async XLA Ops:
  6.5 51.8 %copy-start = (bf16[4,64,4096]{2,1,0:T(8,128)(2,1)S(1)}, bf16[4,64,4096]{2,1,0:T(8,128)(2,1)}, u32[]{:S(2)}) copy-start(bf16[4,64,4096]{2,1,0:T(8,128)(2,1)} %param.8) | copy-start | bytes 6291460
  49.9 6.7 %copy-start.4 = (s32[16]{0:T(128)S(1)}, s32[16]{0:T(128)}, u32[]{:S(2)}) copy-start(s32[16]{0:T(128)} %param.12) | copy-start | bytes 196
  49.9 6.8 %copy-start.3 = (s32[16,16]{1,0:T(8,128)S(1)}, s32[16,16]{1,0:T(8,128)}, u32[]{:S(2)}) copy-start(s32[16,16]{1,0:T(8,128)} %param.11) | copy-start | bytes 3076
  49.9 7.4 %copy-start.5 = (s32[16]{0:T(128)S(1)}, s32[16]{0:T(128)}, u32[]{:S(2)}) copy-start(s32[16]{0:T(128)} %param.13) | copy-start | bytes 196
  49.9 7.5 %copy-start.2 = (bf16[4,64,2,512]{3,2,1,0:T(2,128)(2,1)S(1)}, bf16[4,64,2,512]{3,2,1,0:T(2,128)(2,1)}, u32[]{:S(2)}) copy-start(bf16[4,64,2,512]{3,2,1,0:T(2,128)(2,1)} %param.9) | copy-start | bytes 1572868
  49.9 190.4 %all-to-all-start = ((bf16[8,8,2,128,256]{4,3,2,1,0:T(8,128)(2,1)}), bf16[8,8,2,128,256]{4,3,2,1,0:T(8,128)(2,1)}, u32[]{:S(2)}, u32[]{:S(2)}) async-start(bf16[8,8,2,128,256]{4,3,2,1,0:T(8,128)(2,1)} %bitcast.129), calls=%async_computation | async-start | bytes 16777216 | tf_op jit(solution)/shard_map/all_to_all | solution.py:143
  56.4 303.9 %all-gather.2.cloned.1.call-start = ((), (), s32[]{:S(2)}) async-start(), calls=%async_computation.1 | async-start | bytes 3145728 | tf_op jit(solution)/shard_map/all_gather | solution.py:163
  346.4 17.0 %copy-start.1 = (bf16[4,64,4096]{2,1,0:T(8,128)(2,1)S(1)}, bf16[4,64,4096]{2,1,0:T(8,128)(2,1)}, u32[]{:S(2)}) copy-start(bf16[4,64,4096]{2,1,0:T(8,128)(2,1)} %param.8) | copy-start | bytes 6291460
Sparse Core Ops, SparseCore 0:
  350.7 9.5 all-gather.1
where the time goes:
time: 371 us; the launch traced here: 370 us
  waiting for transfers between devices  191 us (51%)
  local copies, waits for them, and re-layouts  75.7 us (20%)
  matrix products  42.2 us (11%)
  other arithmetic  41.1 us (11%)
  between operations  13.5 us (4%)
  starting transfers between devices  6.68 us (2%)
    all_to_all x1, waiting for transfers between devices, per_device(): lax.all_to_all(outgoing, ('seq', 'sub'), split_axis=0, concat_axis=0, til...  181 us
    gather x4, local copies, waits for them, and re-layouts, one_sequence(): fetched = jnp.take(received, index_row, axis=0)  21.7 us
    gather x1, local copies, waits for them, and re-layouts, per_device(): jnp.take(split_pages, send_slots, axis=0)  20.8 us
    dot_general x4, matrix products, partial_softmax(): jnp.einsum('rkgd,nkd->kgrn', query_heads, cache_keys, preferred_element_t...  18.8 us
    reduce_sum x4, other arithmetic, partial_softmax(): jnp.sum(cache_weights, axis=-1) + jnp.sum(fresh_weights, axis=-1)  17.8 us
    dot_general x4, matrix products, partial_softmax(): jnp.einsum('kgrn,nkd->kgrd', cache_weights.astype(jnp.bfloat16), cache_va...  17.5 us
    reshape x1, local copies, waits for them, and re-layouts, per_device(): split_pages = kv_pages.reshape(pages_dev, 2, PAGE, sub_count, part_width)  12.1 us
    all_gather x1, waiting for transfers between devices, per_device(): return lax.all_gather(own_heads, 'sub', axis=2, tiled=True)  9.72 us
  transfers between devices with their start and end apart: 2, of which 2 were waited for; matrix products, arithmetic and copies ran while one was open for 1% of the time, Pallas kernels for 0%

commit v1 on v0

--- a/solution.py
+++ b/solution.py
@@ -1,6 +1,10 @@
+import functools
+
 import jax
 import jax.numpy as jnp
 from jax import lax
+from jax.experimental import pallas as pl
+from jax.experimental.pallas import tpu as pltpu
 from jax.sharding import PartitionSpec as P
 
 HD = 128
@@ -96,7 +100,7 @@
     )
 
 
-def per_device(queries, new_kv, kv_pages, page_table, cached_len, is_prefill):
+def exchange_pages(queries, new_kv, kv_pages, page_table, cached_len, is_prefill):
     seq_shards = lax.axis_size("seq")
     sub_count = lax.axis_size("sub")
     owners = seq_shards * sub_count
@@ -163,6 +167,447 @@
     return lax.all_gather(own_heads, "sub", axis=2, tiled=True)
 
 
+MESH = pl.DeviceIdType.MESH
+SCALE = HD ** (-0.5)
+
+
+def greet(z, n):
+    has_left, has_right = z > 0, z < n - 1
+    barrier = pltpu.get_barrier_semaphore()
+
+    @pl.when(has_left)
+    def _():
+        pl.semaphore_signal(barrier, inc=1, device_id={"seq": z - 1}, device_id_type=MESH)
+
+    @pl.when(has_right)
+    def _():
+        pl.semaphore_signal(barrier, inc=1, device_id={"seq": z + 1}, device_id_type=MESH)
+
+    pl.semaphore_wait(barrier, has_left.astype(jnp.int32) + has_right.astype(jnp.int32))
+    return has_left, has_right
+
+
+def remote(src, dst, send, recv, z):
+    return pltpu.make_async_remote_copy(
+        src_ref=src, dst_ref=dst, send_sem=send, recv_sem=recv,
+        device_id={"seq": z}, device_id_type=MESH,
+    )
+
+
+def gather_queries_kernel(n, chunks, own, out, rin, rout, lin, lout, rs, rr, ls, lr):
+    z = lax.axis_index("seq")
+    has_left, has_right = greet(z, n)
+    for c, (start, size) in enumerate(chunks):
+        rows = pl.ds(start, size)
+        right = remote(rout.at[rows], rin.at[rows], rs.at[c], rr.at[c], z + 1)
+        left = remote(lout.at[rows], lin.at[rows], ls.at[c], lr.at[c], z - 1)
+
+        @pl.when(has_left)
+        def _():
+            right.wait_recv()
+            rout[rows] = own[rows] + rin[rows]
+
+        @pl.when(jnp.logical_not(has_left))
+        def _():
+            rout[rows] = own[rows]
+
+        @pl.when(has_right)
+        def _():
+            right.start()
+            left.wait_recv()
+            lout[rows] = own[rows] + lin[rows]
+            out[rows] = rout[rows] + lin[rows]
+
+        @pl.when(jnp.logical_not(has_right))
+        def _():
+            lout[rows] = own[rows]
+            out[rows] = rout[rows]
+
+        @pl.when(has_left)
+        def _():
+            left.start()
+
+    for c, (start, size) in enumerate(chunks):
+        rows = pl.ds(start, size)
+
+        @pl.when(has_right)
+        def _():
+            remote(rout.at[rows], rin.at[rows], rs.at[c], rr.at[c], z + 1).wait_send()
+
+        @pl.when(has_left)
+        def _():
+            remote(lout.at[rows], lin.at[rows], ls.at[c], lr.at[c], z - 1).wait_send()
+
+
+def gather_queries(own, n, row_count):
+    total, width = own.shape
+    chunks = []
+    start = 0
+    while start < total:
+        size = min(row_count // 2, total - start)
+        chunks.append((start, size))
+        start += size
+    count = len(chunks)
+    buffer = pltpu.VMEM(own.shape, own.dtype)
+    return pl.pallas_call(
+        functools.partial(gather_queries_kernel, n, chunks),
+        out_shape=jax.ShapeDtypeStruct(own.shape, own.dtype),
+        in_specs=[pl.BlockSpec(memory_space=pltpu.VMEM)],
+        out_specs=pl.BlockSpec(memory_space=pltpu.VMEM),
+        scratch_shapes=[buffer] * 4 + [pltpu.SemaphoreType.DMA((count,))] * 4,
+        compiler_params=pltpu.CompilerParams(collective_id=0, has_side_effects=True),
+        name="gather_queries",
+    )(own)
+
+
+def merge(o1, e1, o2, e2):
+    top = jnp.maximum(e1, e2)
+    w1, w2 = jnp.exp(e1 - top), jnp.exp(e2 - top)
+    total = w1 + w2
+    inv = 1.0 / total
+    return o1 * (w1 * inv) + o2 * (w2 * inv), top + jnp.log(total)
+
+
+def reduce_outputs_kernel(
+    n, parts, heads, o, e, od, ed, out, oute, outd, outed, *scratch
+):
+    rino, rouo, lino, louo, rine, roue, line, loue = scratch[:8]
+    drino, drouo, dlino, dlouo, drine, droue, dline, dloue = scratch[8:16]
+    rs, rr, ls, lr, res, rer, les, ler = scratch[16:]
+    z = lax.axis_index("seq")
+    has_left, has_right = greet(z, n)
+    views = []
+    for c in range(parts + 1):
+        if c == 0:
+            refs = (od, ed, outd, outed, drino, drouo, dlino, dlouo, drine, droue, dline, dloue)
+            views.append(refs)
+        else:
+            refs = (o, e, out, oute, rino, rouo, lino, louo, rine, roue, line, loue)
+            views.append(tuple(r.at[c - 1] for r in refs))
+
+    def copies(c):
+        _, _, _, _, ri, ro, li, lo, rei, reo, lei, leo = views[c]
+        to_right = (
+            remote(ro, ri, rs.at[c], rr.at[c], z + 1),
+            remote(reo, rei, res.at[c], rer.at[c], z + 1),
+        )
+        to_left = (
+            remote(lo, li, ls.at[c], lr.at[c], z - 1),
+            remote(leo, lei, les.at[c], ler.at[c], z - 1),
+        )
+        return to_right, to_left
+
+    def join(o1, e1, o2, e2, oo, eo):
+        for k in range(heads):
+            rows = pl.ds(k * HD, HD)
+            joined, stat = merge(
+                o1[rows].astype(jnp.float32), e1[pl.ds(k, 1)], o2[rows].astype(jnp.float32), e2[pl.ds(k, 1)]
+            )
+            oo[rows] = joined.astype(oo.dtype)
+            eo[pl.ds(k, 1)] = stat
+
+    for c in range(parts + 1):
+        ov, ev, outv, outev, ri, ro, li, lo, rei, reo, lei, leo = views[c]
+        to_right, to_left = copies(c)
+
+        @pl.when(has_left)
+        def _():
+            for x in to_right:
+                x.wait_recv()
+            join(ov, ev, ri, rei, ro, reo)
+
+        @pl.when(jnp.logical_not(has_left))
+        def _():
+            ro[...] = ov[...]
+            reo[...] = ev[...]
+
+        @pl.when(has_right)
+        def _():
+            for x in to_right:
+                x.start()
+            for x in to_left:
+                x.wait_recv()
+            join(ov, ev, li, lei, lo, leo)
+
+        @pl.when(jnp.logical_not(has_right))
+        def _():
+            lo[...] = ov[...]
+            leo[...] = ev[...]
+
+        @pl.when(has_left)
+        def _():
+            for x in to_left:
+                x.start()
+
+        @pl.when(has_right)
+        def _():
+            join(ro, reo, li, lei, outv, outev)
+
+        @pl.when(jnp.logical_not(has_right))
+        def _():
+            outv[...] = ro[...]
+            outev[...] = reo[...]
+
+    for c in range(parts + 1):
+        to_right, to_left = copies(c)
+
+        @pl.when(has_right)
+        def _():
+            for x in to_right:
+                x.wait_send()
+
+        @pl.when(has_left)
+        def _():
+            for x in to_left:
+                x.wait_send()
+
+
+def reduce_outputs(o, e, od, ed, n):
+    parts, heads = e.shape[:2]
+    shapes = [jax.ShapeDtypeStruct(x.shape, x.dtype) for x in (o, e, od, ed)]
+    big = [pltpu.VMEM(o.shape, o.dtype)] * 4 + [pltpu.VMEM(e.shape, e.dtype)] * 4
+    small = [pltpu.VMEM(od.shape, od.dtype)] * 4 + [pltpu.VMEM(ed.shape, ed.dtype)] * 4
+    return pl.pallas_call(
+        functools.partial(reduce_outputs_kernel, n, parts, heads),
+        out_shape=shapes,
+        in_specs=[pl.BlockSpec(memory_space=pltpu.VMEM)] * 4,
+        out_specs=[pl.BlockSpec(memory_space=pltpu.VMEM)] * 4,
+        scratch_shapes=big + small + [pltpu.SemaphoreType.DMA((parts + 1,))] * 8,
+        compiler_params=pltpu.CompilerParams(collective_id=1, has_side_effects=True),
+        name="reduce_outputs",
+    )(o, e, od, ed)
+
+
+def stacked_heads(rows, k, group_size):
+    return jnp.concatenate(
+        [rows[:, (k * group_size + g) * HD : (k * group_size + g + 1) * HD] for g in range(group_size)], axis=0
+    )
+
+
+def scores_of(keys, query):
+    return (
+        lax.dot_general(keys, query, (((1,), (1,)), ((), ())), preferred_element_type=jnp.float32) * SCALE
+    )
+
+
+def partial_outputs(query, blocks):
+    scored = [jnp.where(mask, scores_of(keys, query), NEG_FILL) for keys, _, mask in blocks]
+    peak = functools.reduce(jnp.maximum, [jnp.max(s, axis=0, keepdims=True) for s in scored])
+    acc, total = None, None
+    for s, (_, values, mask) in zip(scored, blocks):
+        weights = jnp.where(mask, jnp.exp(s - peak), 0.0)
+        part = jnp.sum(weights, axis=0, keepdims=True)
+        prod = lax.dot_general(
+            values, weights.astype(jnp.bfloat16), (((0,), (0,)), ((), ())), preferred_element_type=jnp.float32
+        )
+        acc = prod if acc is None else acc + prod
+        total = part if total is None else total + part
+    empty = total == 0.0
+    total = jnp.where(empty, 1.0, total)
+    return acc * (1.0 / total), jnp.where(empty, NEG_FILL, peak + jnp.log(total))
+
+
+def prefill_kernel(most, heads, group_size, pages, valid, home, local, q_ref, *refs):
+    page_refs, (fk_ref, fv_ref, o_ref, e_ref) = refs[:most], refs[most:]
+    j = pl.program_id(0)
+    rows = q_ref.shape[0]
+    lanes = group_size * rows
+    key_id = lax.broadcasted_iota(jnp.int32, (PAGE, 1), 0)
+    fresh_id = lax.broadcasted_iota(jnp.int32, (rows, lanes), 0)
+    lane_row = lax.broadcasted_iota(jnp.int32, (rows, lanes), 1) % rows
+    for k in range(heads):
+        cols = slice(k * HD, (k + 1) * HD)
+        query = stacked_heads(q_ref, k, group_size)
+        blocks = [
+            (ref[0, 0, :, cols], ref[0, 1, :, cols], key_id < valid[j, i]) for i, ref in enumerate(page_refs)
+        ]
+        fresh_mask = (fresh_id <= lane_row) & (home[j] == 1)
+        blocks.append((fk_ref[0, :, cols], fv_ref[0, :, cols], fresh_mask))
+        o, e = partial_outputs(query, blocks)
+        o_ref[0, cols, :] = o.astype(o_ref.dtype)
+        e_ref[0, k : k + 1, :] = e
+
+
+def decode_kernel(most, heads, group_size, seqs, pages, valid, home, local, seq, q_ref, *refs):
+    page_refs, (fk_ref, fv_ref, o_ref, e_ref) = refs[:most], refs[most:]
+    j = pl.program_id(0)
+    lanes = group_size * seqs
+    fresh_rows = 16
+    key_id = lax.broadcasted_iota(jnp.int32, (PAGE, 1), 0)
+    fresh_id = lax.broadcasted_iota(jnp.int32, (fresh_rows, 1), 0)
+    mine = lax.broadcasted_iota(jnp.int32, (1, lanes), 1) % seqs == seq[j]
+
+    @pl.when(j == 0)
+    def _():
+        o_ref[...] = jnp.zeros_like(o_ref)
+        e_ref[...] = jnp.full_like(e_ref, NEG_FILL)
+
+    for k in range(heads):
+        cols = slice(k * HD, (k + 1) * HD)
+        query = stacked_heads(q_ref, k, group_size)
+        blocks = [
+            (ref[0, 0, :, cols], ref[0, 1, :, cols], key_id < valid[j, i]) for i, ref in enumerate(page_refs)
+        ]
+        fresh_mask = fresh_id < home[j]
+        blocks.append((fk_ref[0, :fresh_rows, cols], fv_ref[0, :fresh_rows, cols], fresh_mask))
+        o, e = partial_outputs(query, blocks)
+        o_ref[cols, :] = jnp.where(mine, o, o_ref[cols, :].astype(jnp.float32)).astype(o_ref.dtype)
+        e_ref[k : k + 1, :] = jnp.where(mine, e, e_ref[k : k + 1, :])
+
+
+def finish_kernel(heads, group_size, seqs, slot, flag, first, o_ref, od_ref, out_ref):
+    i = pl.program_id(0)
+    rows = out_ref.shape[1]
+
+    @pl.when(flag[i] == 1)
+    def _():
+        for k in range(heads):
+            turned = o_ref[0, k * HD : (k + 1) * HD, :].astype(jnp.float32).T.astype(out_ref.dtype)
+            for g in range(group_size):
+                h = k * group_size + g
+                out_ref[0, :, h * HD : (h + 1) * HD] = turned[g * rows : (g + 1) * rows]
+
+    @pl.when(flag[i] != 1)
+    def _():
+        top = lax.broadcasted_iota(jnp.int32, (rows, 1), 0) == 0
+        pick = lax.broadcasted_iota(jnp.int32, (seqs, 1), 0) == first[0] + i
+        for k in range(heads):
+            turned = od_ref[k * HD : (k + 1) * HD, :].astype(jnp.float32).T
+            for g in range(group_size):
+                h = k * group_size + g
+                line = jnp.sum(jnp.where(pick, turned[g * seqs : (g + 1) * seqs], 0.0), axis=0, keepdims=True)
+                out_ref[0, :, h * HD : (h + 1) * HD] = jnp.where(top, line, 0.0).astype(out_ref.dtype)
+
+
+def move_queries(queries, new_kv, kv_pages, page_table, cached_len, is_prefill):
+    n = lax.axis_size("seq")
+    sub_count = lax.axis_size("sub")
+    z = lax.axis_index("seq")
+    core = lax.axis_index("sub")
+    seq_dev, row_count, query_width = queries.shape
+    pages_dev, kv_width = kv_pages.shape[0], kv_pages.shape[3]
+    seqs, page_count = page_table.shape
+    owners = n * sub_count
+    most = sub_count * (page_count // owners)
+    slots = seqs // 2
+    group_size = query_width // kv_width
+    part_width, query_part = kv_width // sub_count, query_width // sub_count
+    heads = part_width // HD
+
+    other = (core + 1) % sub_count
+    away = lax.dynamic_slice_in_dim(kv_pages, other * part_width, part_width, 3)
+    here = lax.dynamic_slice_in_dim(kv_pages, core * part_width, part_width, 3)
+    came = lax.ppermute(away, "sub", [(c, (c + 1) % sub_count) for c in range(sub_count)])
+    pool = jnp.concatenate([here, came], axis=0)
+
+    seq_ids = jnp.arange(seqs, dtype=jnp.int32)
+    owner = page_table // pages_dev
+    mine = (page_table >= 0) & (owner // sub_count == z)
+    index = page_table % pages_dev + jnp.where(owner % sub_count == core, 0, pages_dev)
+    rank = jnp.cumsum(mine.astype(jnp.int32), axis=1) - 1
+    picked = mine[:, :, None] & (rank[:, :, None] == jnp.arange(most, dtype=jnp.int32))
+    tokens = jnp.clip(cached_len[:, None] - PAGE * jnp.arange(page_count, dtype=jnp.int32), 0, PAGE)
+    page_rows = jnp.sum(jnp.where(picked, index[:, :, None], 0), axis=1)
+    valid_rows = jnp.sum(jnp.where(picked, tokens[:, :, None], 0), axis=1)
+    flags = is_prefill == 1
+    slot_of = jnp.cumsum(flags.astype(jnp.int32)) - 1
+    place_of = jnp.cumsum((~flags).astype(jnp.int32)) - 1
+    slot_ids = jnp.arange(slots, dtype=jnp.int32)
+    slot_seq = jnp.sum(jnp.where(flags & (slot_of == slot_ids[:, None]), seq_ids, 0), axis=1)
+    rest_ids = jnp.arange(seqs - slots, dtype=jnp.int32)
+    rest_seq = jnp.sum(jnp.where(~flags & (place_of == rest_ids[:, None]), seq_ids, 0), axis=1)
+
+    def tables(which):
+        at_home = (which // seq_dev == z).astype(jnp.int32)
+        return page_rows[which], valid_rows[which], at_home, jnp.where(at_home == 1, which % seq_dev, 0)
+
+    slot_tables, rest_tables = tables(slot_seq), tables(rest_seq)
+    my_queries = lax.dynamic_slice_in_dim(queries, core * query_part, query_part, 2)
+    own_slots = jnp.where((slot_tables[2] == 1)[:, None, None], my_queries[slot_tables[3]], 0)
+    first_rows = jnp.where(
+        (seq_ids // seq_dev == z)[:, None], jnp.tile(my_queries[:, 0], (n, 1)), 0
+    )
+    own = jnp.concatenate([own_slots.reshape(slots * row_count, query_part), first_rows], axis=0)
+    gathered = gather_queries(own.astype(queries.dtype), n, row_count)
+
+    my_fresh = lax.dynamic_slice_in_dim(new_kv, core * part_width, part_width, 3)
+    fresh_keys, fresh_values = my_fresh[:, :, 0], my_fresh[:, :, 1]
+    lanes = group_size * row_count
+    rest_lanes = group_size * seqs
+
+    def page_spec(i):
+        return pl.BlockSpec((1, 2, PAGE, part_width), lambda j, pages, *_: (pages[j, i], 0, 0, 0))
+
+    fresh_spec = pl.BlockSpec(
+        (1, row_count, part_width), lambda j, pages, valid, home, local, *_: (local[j], 0, 0)
+    )
+    o, e = pl.pallas_call(
+        functools.partial(prefill_kernel, most, heads, group_size),
+        grid_spec=pltpu.PrefetchScalarGridSpec(
+            num_scalar_prefetch=4,
+            grid=(slots,),
+            in_specs=[pl.BlockSpec((row_count, query_part), lambda j, *_: (j, 0))]
+            + [page_spec(i) for i in range(most)]
+            + [fresh_spec] * 2,
+            out_specs=[
+                pl.BlockSpec((1, part_width, lanes), lambda j, *_: (j, 0, 0)),
+                pl.BlockSpec((1, heads, lanes), lambda j, *_: (j, 0, 0)),
+            ],
+        ),
+        out_shape=[
+            jax.ShapeDtypeStruct((slots, part_width, lanes), jnp.bfloat16),
+            jax.ShapeDtypeStruct((slots, heads, lanes), jnp.float32),
+        ],
+        name="prefill_attention",
+    )(*slot_tables, gathered, *([pool] * most), fresh_keys, fresh_values)
+    od, ed = pl.pallas_call(
+        functools.partial(decode_kernel, most, heads, group_size, seqs),
+        grid_spec=pltpu.PrefetchScalarGridSpec(
+            num_scalar_prefetch=5,
+            grid=(seqs - slots,),
+            in_specs=[pl.BlockSpec((seqs, query_part), lambda j, *_: (slots * row_count // seqs, 0))]
+            + [page_spec(i) for i in range(most)]
+            + [fresh_spec] * 2,
+            out_specs=[
+                pl.BlockSpec((part_width, rest_lanes), lambda j, *_: (0, 0)),
+                pl.BlockSpec((heads, rest_lanes), lambda j, *_: (0, 0)),
+            ],
+        ),
+        out_shape=[
+            jax.ShapeDtypeStruct((part_width, rest_lanes), jnp.bfloat16),
+            jax.ShapeDtypeStruct((heads, rest_lanes), jnp.float32),
+        ],
+        name="decode_attention",
+    )(*rest_tables, rest_seq, gathered, *([pool] * most), fresh_keys, fresh_values)
+    o, _, od, _ = reduce_outputs(o, e, od, ed, n)
+
+    first_seq = z * seq_dev
+    my_flags = lax.dynamic_slice_in_dim(is_prefill, first_seq, seq_dev, 0)
+    my_slots = jnp.maximum(lax.dynamic_slice_in_dim(slot_of, first_seq, seq_dev, 0), 0)
+    own_heads = pl.pallas_call(
+        functools.partial(finish_kernel, heads, group_size, seqs),
+        grid_spec=pltpu.PrefetchScalarGridSpec(
+            num_scalar_prefetch=3,
+            grid=(seq_dev,),
+            in_specs=[
+                pl.BlockSpec((1, part_width, lanes), lambda i, slot, *_: (slot[i], 0, 0)),
+                pl.BlockSpec((part_width, rest_lanes), lambda i, *_: (0, 0)),
+            ],
+            out_specs=pl.BlockSpec((1, row_count, query_part), lambda i, *_: (i, 0, 0)),
+        ),
+        out_shape=jax.ShapeDtypeStruct((seq_dev, row_count, query_part), jnp.bfloat16),
+        name="finish",
+    )(my_slots, my_flags, jnp.reshape(first_seq, (1,)).astype(jnp.int32), o, od)
+    return lax.all_gather(own_heads, "sub", axis=2, tiled=True)
+
+
+def per_device(queries, new_kv, kv_pages, page_table, cached_len, is_prefill):
+    owners = lax.axis_size("seq") * lax.axis_size("sub")
+    if page_table.shape[1] >= owners:
+        return move_queries(queries, new_kv, kv_pages, page_table, cached_len, is_prefill)
+    return exchange_pages(queries, new_kv, kv_pages, page_table, cached_len, is_prefill)
+
+
 def solution(mesh):
     placed = (
         P(("groups", "seq"), None, "head"),

time: 371 us -> 793 us (2.14)
  Pallas kernels: 0 us -> 741 us
  waiting for transfers between devices: 191 us -> 8.09 us
  local copies, waits for them, and re-layouts: 75.7 us -> 18.2 us
  matrix products: 42.2 us -> 0 us
  other arithmetic: 41.1 us -> 11.1 us
    pallas_call x0 -> x5, Pallas kernels: none -> 741 us  [the longest x1 418 us: gather_queries(): pl.pallas_call(functools.partial(gather_queries_kernel, n, chunks), out_s...]
    all_to_all x1 -> x0, waiting for transfers between devices: 181 us -> none  [per_device(): lax.all_to_all(outgoing, ('seq', 'sub'), split_axis=0, concat_axis=0, til...]
    dot_general x16 -> x0, matrix products: 42.2 us -> none  [the longest x4 18.8 us: partial_softmax(): jnp.einsum('rkgd,nkd->kgrn', query_heads, cache_keys, preferred_element_t...]
    gather x5, local copies, waits for them, and re-layouts: 42.5 us -> 6.55 us  [the longest x2 2.28 us: tables(): page_rows[which]]
    reduce_sum x10 -> x3, other arithmetic: 18.7 us -> 0.46 us  [the longest x1 0.22 us: move_queries(): valid_rows = jnp.sum(jnp.where(picked, tokens[:, :, None], 0), axis=1)]
    select_n x13 -> x4, other arithmetic: 15.5 us -> 2.44 us  [the longest x1 1.8 us: move_queries(): jnp.where((slot_tables[2] == 1)[:, None, None], my_queries[slot_tables[3]...]
    reshape x2 -> x0, local copies, waits for them, and re-layouts: 12.2 us -> none  [the longest x1 12.1 us: per_device(): split_pages = kv_pages.reshape(pages_dev, 2, PAGE, sub_count, part_width)]
  transfers between devices with their start and end apart: 2 -> 2, of which waited for: 2 -> 1; matrix products, arithmetic and copies ran while one was open for 1% -> 2% of each run, Pallas kernels for 0% -> 53%
where the time goes in v1:
time: 793 us; the launch traced here: 792 us
  Pallas kernels  741 us (93%)
  local copies, waits for them, and re-layouts  18.2 us (2%)
  between operations  13.6 us (2%)
  other arithmetic  11.1 us (1%)
  waiting for transfers between devices  8.09 us (1%)
    pallas_call x1, Pallas kernels, gather_queries(): pl.pallas_call(functools.partial(gather_queries_kernel, n, chunks), out_s...  418 us
    pallas_call x1, Pallas kernels, reduce_outputs(): pl.pallas_call(functools.partial(reduce_outputs_kernel, n, parts, heads),...  291 us
    pallas_call x1, Pallas kernels, move_queries(): pl.pallas_call(functools.partial(prefill_kernel, most, heads, group_size)...  17.2 us
  transfers between devices with their start and end apart: 2, of which 1 were waited for; matrix products, arithmetic and copies ran while one was open for 2% of the time, Pallas kernels for 53%

profile of v1, /device:TPU:0, one launch (start us, length us, event | category | flops | bytes accessed | tf_op | source)
XLA Modules:
  0.0 792.4 jit_solution(4911352098902071817)
XLA Ops:
  6.6 5.9 constant_dynamic-slice_fusion.4
  12.4 0.5 collective-permute-start
  12.9 0.1 copy.13
  13.0 0.1 fusion.14
  13.3 0.1 add_reduce_fusion
  13.4 0.2 reduce_window_sum.20
  13.7 0.2 select_reduce_fusion
  13.9 0.1 copy.14
  14.0 0.1 select_reduce_fusion.3
  14.1 0.1 select_reduce_fusion.2.seq
  14.3 0.1 copy.15
  14.4 1.1 gather_fusion.3
  15.5 1.1 gather_fusion.4
  16.6 1.1 gather_fusion.1
  17.8 1.1 gather_fusion
  19.0 0.1 broadcast_in_dim.91
  19.3 2.0 gather_fusion.2
  21.4 1.8 bitcast_select_fusion
  23.2 1.5 pad_maximum_fusion.1.own
  24.7 418.5 %gather_queries.1.q_ref = bf16[528,2048]{1,0:T(8,128)(2,1)} custom-call(bf16[528,2048]{1,0:T(8,128)(2,1)} %pad_maximum_fusion.1.own), custom_call_target="tpu_custom_call" | custom-call | tf_op jit(solution)/shard_map/gather_queries/pallas_call | solution.py:252
  443.2 0.6 dynamic_slice.19.flag
  443.8 0.6 maximum_reduce_fusion.slot
  444.4 0.6 constant_dynamic-slice_fusion.2
  445.1 0.5 compare_select_fusion.2
  445.6 0.8 copy_bitcast_fusion
  446.4 5.5 pad_maximum_fusion.refs_0_.refs_1_.refs_2_.refs_3_
  451.9 17.2 %prefill_attention.1 = (bf16[8,256,512]{2,1,0:T(8,128)(2,1)}, f32[8,2,512]{2,1,0:T(2,128)}) custom-call(s32[8,4]{1,0:T(8,128)} %gather_fusion, s32[8,4]{1,0:T(8,128)} %gather_fusion.1, s32[8]{0:T(128)} %copy-done.4, s32[8]{0:T(128)} %get-tuple-element.37.local, bf16[528,2048]{1,0:T(8,128)(2,1)} %gather_queries.1.q_ref, ...), custom_call_target="tpu_custom_call" | custom-call | tf_op jit(solution)/shard_map/prefill_attention/pallas_call | solution.py:544
  469.1 10.1 %decode_attention.1 = (bf16[256,128]{1,0:T(8,128)(2,1)}, f32[2,128]{1,0:T(2,128)}) custom-call(s32[8,4]{1,0:T(8,128)} %gather_fusion.3, s32[8,4]{1,0:T(8,128)} %gather_fusion.4, s32[8]{0:T(128)} %get-tuple-element.20.home, s32[8]{0:T(128)} %get-tuple-element.19.local, s32[8]{0:T(128)} %copy-done.3, bf16[528,2048]{1,0:T(8,128)(2,1)} %gather_queries.1.q_ref, ...), custom_call_target="tpu_custom_call" | custom-call | tf_op jit(solution)/shard_map/decode_attention/pallas_call | solution.py:563
  479.2 290.8 %reduce_outputs.1 = (bf16[8,256,512]{2,1,0:T(8,128)(2,1)}, f32[8,2,512]{2,1,0:T(2,128)}, bf16[256,128]{1,0:T(8,128)(2,1)}, f32[2,128]{1,0:T(2,128)}) custom-call(bf16[8,256,512]{2,1,0:T(8,128)(2,1)} %get-tuple-element.11.o, f32[8,2,512]{2,1,0:T(2,128)} %get-tuple-element.12.e, bf16[256,128]{1,0:T(8,128)(2,1)} %get-tuple-element.13.od, ...), custom_call_target="tpu_custom_call" | custom-call | tf_op jit(solution)/shard_map/reduce_outputs/pallas_call | solution.py:370
  770.0 4.3 finish.1
  774.3 8.1 %all-gather.2.cloned.1.call-done = bf16[4,64,4096]{2,1,0:T(8,128)(2,1)} async-done(((bf16[4,64,2048]{2,1,0:T(8,128)(2,1)}), bf16[4,64,4096]{2,1,0:T(8,128)(2,1)}) %all-gather.2.cloned.1.call-update) | async-done | bytes 2097168 | tf_op jit(solution)/shard_map/all_gather | solution.py:601
  782.4 3.1 copy.29
  (38 shorter events, 0.7 us)
Async XLA Ops:
  6.5 12.6 %copy-start = (bf16[4,64,4096]{2,1,0:T(8,128)(2,1)S(1)}, bf16[4,64,4096]{2,1,0:T(8,128)(2,1)}, u32[]{:S(2)}) copy-start(bf16[4,64,4096]{2,1,0:T(8,128)(2,1)} %param.6) | copy-start | bytes 6291460
  6.5 775.8 %all-gather.2.cloned.1.call-start = ((), (), s32[]{:S(2)}) async-start(), calls=%async_computation | async-start | bytes 3145728 | tf_op jit(solution)/shard_map/all_gather | solution.py:601
  6.5 6.4 copy-start.6
  6.5 6.9 copy-start.2
  6.5 7.1 copy-start.5
  12.4 434.0 %collective-permute-start = (bf16[21,2,128,256]{3,2,1,0:T(8,128)(2,1)}, bf16[21,2,128,256]{3,2,1,0:T(8,128)(2,1)}, u32[]{:S(2)}, u32[]{:S(2)}) collective-permute-start(bf16[21,2,128,256]{3,2,1,0:T(8,128)(2,1)} %get-tuple-element.26), channel_id=1, source_target_pairs={{0,1},{1,0},{2,3},{3,2},{4,5},{5,4},{6,7},{7,6},{8,9},{9,8},{10,11... | collective-permute-start | bytes 8257544 | tf_op jit(solution)/shard_map/ppermute | solution.py:500
  14.2 430.8 %copy-start.3 = (s32[8]{0:T(128)}, s32[8]{0:T(128)S(1)}, u32[]{:S(2)}) copy-start(s32[8]{0:T(128)S(1)} %select_reduce_fusion.2.seq) | copy-start | bytes 100
  18.9 426.1 %copy-start.4 = (s32[8]{0:T(128)}, s32[8]{0:T(128)S(1)}, u32[]{:S(2)}) copy-start(s32[8]{0:T(128)S(1)} %get-tuple-element.22.home) | copy-start | bytes 100
  24.7 419.7 %copy-start.1 = (bf16[4,64,2,512]{3,2,1,0:T(2,128)(2,1)S(1)}, bf16[4,64,2,512]{3,2,1,0:T(2,128)(2,1)}, u32[]{:S(2)}) copy-start(bf16[4,64,2,512]{3,2,1,0:T(2,128)(2,1)} %param.7) | copy-start | bytes 1572868
Sparse Core Ops, SparseCore 0:
  774.4 7.9 all-gather.1

commit v2 on v1

--- a/solution.py
+++ b/solution.py
@@ -194,70 +194,102 @@
     )
 
 
-def gather_queries_kernel(n, chunks, own, out, rin, rout, lin, lout, rs, rr, ls, lr):
+LAG = 2
+
+
+def line_steps(z, n, count, has_left, has_right, from_left, from_right, last):
+    def guarded(c, work):
+        @pl.when((c >= 0) & (c < count))
+        def _():
+            work(c)
+
+    def step(s, carry):
+        guarded(s - LAG * z, from_left)
+        guarded(s - LAG * (n - 1 - z), from_right)
+        guarded(s - LAG * jnp.maximum(z, n - 1 - z), last)
+        return carry
+
+    lax.fori_loop(0, count + LAG * (n - 1), step, 0)
+
+
+def gather_queries_kernel(n, count, own, out, rin, rout, lin, lout, rs, rr, ls, lr):
     z = lax.axis_index("seq")
     has_left, has_right = greet(z, n)
-    for c, (start, size) in enumerate(chunks):
-        rows = pl.ds(start, size)
-        right = remote(rout.at[rows], rin.at[rows], rs.at[c], rr.at[c], z + 1)
-        left = remote(lout.at[rows], lin.at[rows], ls.at[c], lr.at[c], z - 1)
-
+
+    def right(c):
+        return remote(rout.at[c], rin.at[c], rs.at[c], rr.at[c], z + 1)
+
+    def left(c):
+        return remote(lout.at[c], lin.at[c], ls.at[c], lr.at[c], z - 1)
+
+    def from_left(c):
         @pl.when(has_left)
         def _():
-            right.wait_recv()
-            rout[rows] = own[rows] + rin[rows]
+            right(c).wait_recv()
+            rout[c] = own[c] + rin[c]
 
         @pl.when(jnp.logical_not(has_left))
         def _():
-            rout[rows] = own[rows]
-
-        @pl.when(has_right)
-        def _():
-            right.start()
-            left.wait_recv()
-            lout[rows] = own[rows] + lin[rows]
-            out[rows] = rout[rows] + lin[rows]
+            rout[c] = own[c]
+
+        @pl.when(has_right)
+        def _():
+            right(c).start()
+
+    def from_right(c):
+        @pl.when(has_right)
+        def _():
+            left(c).wait_recv()
+            lout[c] = own[c] + lin[c]
 
         @pl.when(jnp.logical_not(has_right))
         def _():
-            lout[rows] = own[rows]
-            out[rows] = rout[rows]
+            lout[c] = own[c]
 
         @pl.when(has_left)
         def _():
-            left.start()
-
-    for c, (start, size) in enumerate(chunks):
-        rows = pl.ds(start, size)
-
-        @pl.when(has_right)
-        def _():
-            remote(rout.at[rows], rin.at[rows], rs.at[c], rr.at[c], z + 1).wait_send()
+            left(c).start()
+
+    def last(c):
+        @pl.when(has_right)
+        def _():
+            out[c] = rout[c] + lin[c]
+
+        @pl.when(jnp.logical_not(has_right))
+        def _():
+            out[c] = rout[c]
+
+    line_steps(z, n, count, has_left, has_right, from_left, from_right, last)
+
+    def drain(c, carry):
+        @pl.when(has_right)
+        def _():
+            right(c).wait_send()
 
         @pl.when(has_left)
         def _():
-            remote(lout.at[rows], lin.at[rows], ls.at[c], lr.at[c], z - 1).wait_send()
-
-
-def gather_queries(own, n, row_count):
+            left(c).wait_send()
+
+        return carry
+
+    lax.fori_loop(0, count, drain, 0)
+
+
+def gather_queries(own, n):
     total, width = own.shape
-    chunks = []
-    start = 0
-    while start < total:
-        size = min(row_count // 2, total - start)
-        chunks.append((start, size))
-        start += size
-    count = len(chunks)
-    buffer = pltpu.VMEM(own.shape, own.dtype)
+    rows = 48 if total % 48 == 0 else 16
+    count = total // rows
+    shape = (count, rows, width)
+    buffer = pltpu.VMEM(shape, own.dtype)
     return pl.pallas_call(
-        functools.partial(gather_queries_kernel, n, chunks),
-        out_shape=jax.ShapeDtypeStruct(own.shape, own.dtype),
+        functools.partial(gather_queries_kernel, n, count),
+        out_shape=jax.ShapeDtypeStruct(shape, own.dtype),
         in_specs=[pl.BlockSpec(memory_space=pltpu.VMEM)],
         out_specs=pl.BlockSpec(memory_space=pltpu.VMEM),
         scratch_shapes=[buffer] * 4 + [pltpu.SemaphoreType.DMA((count,))] * 4,
         compiler_params=pltpu.CompilerParams(collective_id=0, has_side_effects=True),
         name="gather_queries",
-    )(own)
+    )(own.reshape(shape)).reshape(total, width)
 
 
 def merge(o1, e1, o2, e2):
@@ -269,113 +301,103 @@
 
 
 def reduce_outputs_kernel(
-    n, parts, heads, o, e, od, ed, out, oute, outd, outed, *scratch
+    n, count, o, e, out, oute, ri, ro, li, lo, rei, reo, lei, leo, rs, rr, ls, lr, res, rer, les, ler
 ):
-    rino, rouo, lino, louo, rine, roue, line, loue = scratch[:8]
-    drino, drouo, dlino, dlouo, drine, droue, dline, dloue = scratch[8:16]
-    rs, rr, ls, lr, res, rer, les, ler = scratch[16:]
     z = lax.axis_index("seq")
     has_left, has_right = greet(z, n)
-    views = []
-    for c in range(parts + 1):
-        if c == 0:
-            refs = (od, ed, outd, outed, drino, drouo, dlino, dlouo, drine, droue, dline, dloue)
-            views.append(refs)
-        else:
-            refs = (o, e, out, oute, rino, rouo, lino, louo, rine, roue, line, loue)
-            views.append(tuple(r.at[c - 1] for r in refs))
-
-    def copies(c):
-        _, _, _, _, ri, ro, li, lo, rei, reo, lei, leo = views[c]
-        to_right = (
-            remote(ro, ri, rs.at[c], rr.at[c], z + 1),
-            remote(reo, rei, res.at[c], rer.at[c], z + 1),
+
+    def right(c):
+        return (
+            remote(ro.at[c], ri.at[c], rs.at[c], rr.at[c], z + 1),
+            remote(reo.at[c], rei.at[c], res.at[c], rer.at[c], z + 1),
         )
-        to_left = (
-            remote(lo, li, ls.at[c], lr.at[c], z - 1),
-            remote(leo, lei, les.at[c], ler.at[c], z - 1),
+
+    def left(c):
+        return (
+            remote(lo.at[c], li.at[c], ls.at[c], lr.at[c], z - 1),
+            remote(leo.at[c], lei.at[c], les.at[c], ler.at[c], z - 1),
         )
-        return to_right, to_left
-
-    def join(o1, e1, o2, e2, oo, eo):
-        for k in range(heads):
-            rows = pl.ds(k * HD, HD)
-            joined, stat = merge(
-                o1[rows].astype(jnp.float32), e1[pl.ds(k, 1)], o2[rows].astype(jnp.float32), e2[pl.ds(k, 1)]
-            )
-            oo[rows] = joined.astype(oo.dtype)
-            eo[pl.ds(k, 1)] = stat
-
-    for c in range(parts + 1):
-        ov, ev, outv, outev, ri, ro, li, lo, rei, reo, lei, leo = views[c]
-        to_right, to_left = copies(c)
-
+
+    def join(o1, e1, o2, e2, oo, eo, c):
+        joined, stat = merge(o1[c].astype(jnp.float32), e1[c], o2[c].astype(jnp.float32), e2[c])
+        oo[c] = joined.astype(oo.dtype)
+        eo[c] = stat
+
+    def from_left(c):
         @pl.when(has_left)
         def _():
-            for x in to_right:
+            for x in right(c):
                 x.wait_recv()
-            join(ov, ev, ri, rei, ro, reo)
+            join(o, e, ri, rei, ro, reo, c)
 
         @pl.when(jnp.logical_not(has_left))
         def _():
-            ro[...] = ov[...]
-            reo[...] = ev[...]
-
-        @pl.when(has_right)
-        def _():
-            for x in to_right:
+            ro[c] = o[c]
+            reo[c] = e[c]
+
+        @pl.when(has_right)
+        def _():
+            for x in right(c):
                 x.start()
-            for x in to_left:
+
+    def from_right(c):
+        @pl.when(has_right)
+        def _():
+            for x in left(c):
                 x.wait_recv()
-            join(ov, ev, li, lei, lo, leo)
+            join(o, e, li, lei, lo, leo, c)
 
         @pl.when(jnp.logical_not(has_right))
         def _():
-            lo[...] = ov[...]
-            leo[...] = ev[...]
+            lo[c] = o[c]
+            leo[c] = e[c]
 
         @pl.when(has_left)
         def _():
-            for x in to_left:
+            for x in left(c):
                 x.start()
 
-        @pl.when(has_right)
-        def _():
-            join(ro, reo, li, lei, outv, outev)
+    def last(c):
+        @pl.when(has_right)
+        def _():
+            join(ro, reo, li, lei, out, oute, c)
 
         @pl.when(jnp.logical_not(has_right))
         def _():
-            outv[...] = ro[...]
-            outev[...] = reo[...]
-
-    for c in range(parts + 1):
-        to_right, to_left = copies(c)
-
-        @pl.when(has_right)
-        def _():
-            for x in to_right:
+            out[c] = ro[c]
+            oute[c] = reo[c]
+
+    line_steps(z, n, count, has_left, has_right, from_left, from_right, last)
+
+    def drain(c, carry):
+        @pl.when(has_right)
+        def _():
+            for x in right(c):
                 x.wait_send()
 
         @pl.when(has_left)
         def _():
-            for x in to_left:
+            for x in left(c):
                 x.wait_send()
 
-
-def reduce_outputs(o, e, od, ed, n):
-    parts, heads = e.shape[:2]
-    shapes = [jax.ShapeDtypeStruct(x.shape, x.dtype) for x in (o, e, od, ed)]
-    big = [pltpu.VMEM(o.shape, o.dtype)] * 4 + [pltpu.VMEM(e.shape, e.dtype)] * 4
-    small = [pltpu.VMEM(od.shape, od.dtype)] * 4 + [pltpu.VMEM(ed.shape, ed.dtype)] * 4
+        return carry
+
+    lax.fori_loop(0, count, drain, 0)
+
+
+def reduce_outputs(o, e, n):
+    count = e.shape[0]
     return pl.pallas_call(
-        functools.partial(reduce_outputs_kernel, n, parts, heads),
-        out_shape=shapes,
-        in_specs=[pl.BlockSpec(memory_space=pltpu.VMEM)] * 4,
-        out_specs=[pl.BlockSpec(memory_space=pltpu.VMEM)] * 4,
-        scratch_shapes=big + small + [pltpu.SemaphoreType.DMA((parts + 1,))] * 8,
+        functools.partial(reduce_outputs_kernel, n, count),
+        out_shape=[jax.ShapeDtypeStruct(x.shape, x.dtype) for x in (o, e)],
+        in_specs=[pl.BlockSpec(memory_space=pltpu.VMEM)] * 2,
+        out_specs=[pl.BlockSpec(memory_space=pltpu.VMEM)] * 2,
+        scratch_shapes=[pltpu.VMEM(o.shape, o.dtype)] * 4
+        + [pltpu.VMEM(e.shape, e.dtype)] * 4
+        + [pltpu.SemaphoreType.DMA((count,))] * 8,
         compiler_params=pltpu.CompilerParams(collective_id=1, has_side_effects=True),
         name="reduce_outputs",
-    )(o, e, od, ed)
+    )(o, e)[0]
 
 
 def stacked_heads(rows, k, group_size):
@@ -424,12 +446,12 @@
         fresh_mask = (fresh_id <= lane_row) & (home[j] == 1)
         blocks.append((fk_ref[0, :, cols], fv_ref[0, :, cols], fresh_mask))
         o, e = partial_outputs(query, blocks)
-        o_ref[0, cols, :] = o.astype(o_ref.dtype)
-        e_ref[0, k : k + 1, :] = e
+        o_ref[k] = o.astype(o_ref.dtype)
+        e_ref[k] = e
 
 
 def decode_kernel(most, heads, group_size, seqs, pages, valid, home, local, seq, q_ref, *refs):
-    page_refs, (fk_ref, fv_ref, o_ref, e_ref) = refs[:most], refs[most:]
+    page_refs, (fk_ref, fv_ref, _, _, o_ref, e_ref) = refs[:most], refs[most:]
     j = pl.program_id(0)
     lanes = group_size * seqs
     fresh_rows = 16
@@ -451,8 +473,9 @@
         fresh_mask = fresh_id < home[j]
         blocks.append((fk_ref[0, :fresh_rows, cols], fv_ref[0, :fresh_rows, cols], fresh_mask))
         o, e = partial_outputs(query, blocks)
-        o_ref[cols, :] = jnp.where(mine, o, o_ref[cols, :].astype(jnp.float32)).astype(o_ref.dtype)
-        e_ref[k : k + 1, :] = jnp.where(mine, e, e_ref[k : k + 1, :])
+        place = slice(k * lanes, (k + 1) * lanes)
+        o_ref[0, :, place] = jnp.where(mine, o, o_ref[0, :, place].astype(jnp.float32)).astype(o_ref.dtype)
+        e_ref[0, :, place] = jnp.where(mine, e, e_ref[0, :, place])
 
 
 def finish_kernel(heads, group_size, seqs, slot, flag, first, o_ref, od_ref, out_ref):
@@ -462,7 +485,7 @@
     @pl.when(flag[i] == 1)
     def _():
         for k in range(heads):
-            turned = o_ref[0, k * HD : (k + 1) * HD, :].astype(jnp.float32).T.astype(out_ref.dtype)
+            turned = o_ref[k].astype(jnp.float32).T.astype(out_ref.dtype)
             for g in range(group_size):
                 h = k * group_size + g
                 out_ref[0, :, h * HD : (h + 1) * HD] = turned[g * rows : (g + 1) * rows]
@@ -472,7 +495,8 @@
         top = lax.broadcasted_iota(jnp.int32, (rows, 1), 0) == 0
         pick = lax.broadcasted_iota(jnp.int32, (seqs, 1), 0) == first[0] + i
         for k in range(heads):
-            turned = od_ref[k * HD : (k + 1) * HD, :].astype(jnp.float32).T
+            place = slice(k * seqs * group_size, (k + 1) * seqs * group_size)
+            turned = od_ref[0, :, place].astype(jnp.float32).T
             for g in range(group_size):
                 h = k * group_size + g
                 line = jnp.sum(jnp.where(pick, turned[g * seqs : (g + 1) * seqs], 0.0), axis=0, keepdims=True)
@@ -528,12 +552,12 @@
         (seq_ids // seq_dev == z)[:, None], jnp.tile(my_queries[:, 0], (n, 1)), 0
     )
     own = jnp.concatenate([own_slots.reshape(slots * row_count, query_part), first_rows], axis=0)
-    gathered = gather_queries(own.astype(queries.dtype), n, row_count)
+    gathered = gather_queries(own.astype(queries.dtype), n)
 
     my_fresh = lax.dynamic_slice_in_dim(new_kv, core * part_width, part_width, 3)
     fresh_keys, fresh_values = my_fresh[:, :, 0], my_fresh[:, :, 1]
     lanes = group_size * row_count
-    rest_lanes = group_size * seqs
+    count = slots * heads + 1
 
     def page_spec(i):
         return pl.BlockSpec((1, 2, PAGE, part_width), lambda j, pages, *_: (pages[j, i], 0, 0, 0))
@@ -550,36 +574,35 @@
             + [page_spec(i) for i in range(most)]
             + [fresh_spec] * 2,
             out_specs=[
-                pl.BlockSpec((1, part_width, lanes), lambda j, *_: (j, 0, 0)),
-                pl.BlockSpec((1, heads, lanes), lambda j, *_: (j, 0, 0)),
+                pl.BlockSpec((heads, HD, lanes), lambda j, *_: (j, 0, 0)),
+                pl.BlockSpec((heads, 1, lanes), lambda j, *_: (j, 0, 0)),
             ],
         ),
         out_shape=[
-            jax.ShapeDtypeStruct((slots, part_width, lanes), jnp.bfloat16),
-            jax.ShapeDtypeStruct((slots, heads, lanes), jnp.float32),
+            jax.ShapeDtypeStruct((count, HD, lanes), jnp.bfloat16),
+            jax.ShapeDtypeStruct((count, 1, lanes), jnp.float32),
         ],
         name="prefill_attention",
     )(*slot_tables, gathered, *([pool] * most), fresh_keys, fresh_values)
-    od, ed = pl.pallas_call(
+    o, e = pl.pallas_call(
         functools.partial(decode_kernel, most, heads, group_size, seqs),
         grid_spec=pltpu.PrefetchScalarGridSpec(
             num_scalar_prefetch=5,
             grid=(seqs - slots,),
             in_specs=[pl.BlockSpec((seqs, query_part), lambda j, *_: (slots * row_count // seqs, 0))]
             + [page_spec(i) for i in range(most)]
-            + [fresh_spec] * 2,
+            + [fresh_spec] * 2
+            + [pl.BlockSpec(memory_space=pl.ANY)] * 2,
             out_specs=[
-                pl.BlockSpec((part_width, rest_lanes), lambda j, *_: (0, 0)),
-                pl.BlockSpec((heads, rest_lanes), lambda j, *_: (0, 0)),
+                pl.BlockSpec((1, HD, lanes), lambda j, *_: (count - 1, 0, 0)),
+                pl.BlockSpec((1, 1, lanes), lambda j, *_: (count - 1, 0, 0)),
             ],
         ),
-        out_shape=[
-            jax.ShapeDtypeStruct((part_width, rest_lanes), jnp.bfloat16),
-            jax.ShapeDtypeStruct((heads, rest_lanes), jnp.float32),
-        ],
+        out_shape=[jax.ShapeDtypeStruct(x.shape, x.dtype) for x in (o, e)],
+        input_output_aliases={8 + most: 0, 9 + most: 1},
         name="decode_attention",
-    )(*rest_tables, rest_seq, gathered, *([pool] * most), fresh_keys, fresh_values)
-    o, _, od, _ = reduce_outputs(o, e, od, ed, n)
+    )(*rest_tables, rest_seq, gathered, *([pool] * most), fresh_keys, fresh_values, o, e)
+    o = reduce_outputs(o, e, n)
 
     first_seq = z * seq_dev
     my_flags = lax.dynamic_slice_in_dim(is_prefill, first_seq, seq_dev, 0)
@@ -590,14 +613,14 @@
             num_scalar_prefetch=3,
             grid=(seq_dev,),
             in_specs=[
-                pl.BlockSpec((1, part_width, lanes), lambda i, slot, *_: (slot[i], 0, 0)),
-                pl.BlockSpec((part_width, rest_lanes), lambda i, *_: (0, 0)),
+                pl.BlockSpec((heads, HD, lanes), lambda i, slot, *_: (slot[i], 0, 0)),
+                pl.BlockSpec((1, HD, lanes), lambda i, *_: (count - 1, 0, 0)),
             ],
             out_specs=pl.BlockSpec((1, row_count, query_part), lambda i, *_: (i, 0, 0)),
         ),
         out_shape=jax.ShapeDtypeStruct((seq_dev, row_count, query_part), jnp.bfloat16),
         name="finish",
-    )(my_slots, my_flags, jnp.reshape(first_seq, (1,)).astype(jnp.int32), o, od)
+    )(my_slots, my_flags, jnp.reshape(first_seq, (1,)).astype(jnp.int32), o, o)
     return lax.all_gather(own_heads, "sub", axis=2, tiled=True)
 
 

time: 793 us -> 218 us (0.27)
  Pallas kernels: 741 us -> 165 us
    pallas_call x2, Pallas kernels: 709 us -> 133 us  [the longest x1 68.8 us: gather_queries(): pl.pallas_call(functools.partial(gather_queries_kernel, n, count), out_sh...]
  transfers between devices with their start and end apart: 2 -> 2, of which waited for: 1 -> 1; matrix products, arithmetic and copies ran while one was open for 2% -> 7% of each run, Pallas kernels for 53% -> 32%
where the time goes in v2:
time: 218 us
  Pallas kernels  165 us (76%)
  local copies, waits for them, and re-layouts  18.2 us (8%)
  between operations  13.5 us (6%)
  other arithmetic  11.1 us (5%)
  waiting for transfers between devices  9.84 us (5%)
    pallas_call x1, Pallas kernels, gather_queries(): pl.pallas_call(functools.partial(gather_queries_kernel, n, count), out_sh...  68.8 us
    pallas_call x1, Pallas kernels, reduce_outputs(): pl.pallas_call(functools.partial(reduce_outputs_kernel, n, count), out_sh...  64.5 us
    pallas_call x1, Pallas kernels, move_queries(): pl.pallas_call(functools.partial(prefill_kernel, most, heads, group_size)...  17.5 us
    pallas_call x1, Pallas kernels, move_queries(): pl.pallas_call(functools.partial(decode_kernel, most, heads, group_size,...  10.2 us
    all_gather x1, waiting for transfers between devices, move_queries(): return lax.all_gather(own_heads, 'sub', axis=2, tiled=True)  9.82 us
    dynamic_slice x1, local copies, waits for them, and re-layouts, move_queries(): here = lax.dynamic_slice_in_dim(kv_pages, core * part_width, part_width, 3)  5.85 us
    concatenate x1, other arithmetic, move_queries(): pool = jnp.concatenate([here, came], axis=0)  5.47 us
  transfers between devices with their start and end apart: 2, of which 1 were waited for; matrix products, arithmetic and copies ran while one was open for 7% of the time, Pallas kernels for 32%

profile of v2, /device:TPU:0, one launch (start us, length us, event | category | flops | bytes accessed | tf_op | source)
XLA Modules:
  0.0 217.7 jit_solution(1043929716536964604)
XLA Ops:
  6.6 5.9 %constant_dynamic-slice_fusion.4 = (bf16[21,2,128,256]{3,2,1,0:T(8,128)(2,1)}, bf16[21,2,128,256]{3,2,1,0:T(8,128)(2,1)}) fusion(bf16[21,2,128,512]{3,2,1,0:T(8,128)(2,1)} %param.8, s32[]{:T(128)S(6)} %select_n.179, s32[]{:T(128)S(6)} %select_n.181), kind=kLoop, calls=%fused_computation.65 | loop fusion | bytes 11010056 | tf_op jit(solution)/shard_map/dynamic_slice | solution.py:523
  12.4 0.5 collective-permute-start
  12.9 0.1 copy.15
  13.0 0.1 fusion.14
  13.3 0.1 add_reduce_fusion
  13.4 0.2 reduce_window_sum.20
  13.7 0.2 select_reduce_fusion
  13.9 0.1 copy.17
  14.0 0.1 select_reduce_fusion.2
  14.1 0.1 select_reduce_fusion.3.seq
  14.3 0.1 copy.18
  14.4 1.1 gather_fusion.3
  15.5 1.1 gather_fusion.4
  16.6 1.1 gather_fusion.1
  17.8 1.1 gather_fusion
  18.9 0.6 compare_select_fusion.3
  19.6 0.1 broadcast_in_dim.92
  19.9 2.0 gather_fusion.2
  22.0 1.8 bitcast_select_fusion
  23.8 1.5 pad_maximum_fusion.1
  25.3 68.8 %gather_queries.1 = bf16[11,48,2048]{2,1,0:T(8,128)(2,1)} custom-call(bf16[11,48,2048]{2,1,0:T(8,128)(2,1)} %bitcast.42), custom_call_target="tpu_custom_call" | custom-call | tf_op jit(solution)/shard_map/gather_queries/pallas_call | solution.py:284
  94.1 0.6 dynamic_slice.19.flag
  94.8 0.6 maximum_reduce_fusion.slot
  95.4 0.6 constant_dynamic-slice_fusion.2
  96.0 0.7 copy_bitcast_fusion
  96.8 5.5 %pad_maximum_fusion.refs_0_.refs_1_.refs_2_.refs_3_ = bf16[42,2,128,256]{3,2,1,0:T(8,128)(2,1)} fusion(bf16[21,2,128,256]{3,2,1,0:T(8,128)(2,1)} %collective-permute-done, bf16[21,2,128,256]{3,2,1,0:T(8,128)(2,1)} %get-tuple-element.23), kind=kLoop, calls=%fused_computation.5 | loop fusion | flops 2752512 | bytes 11010048 | tf_op jit(solution)/shard_map/concatenate | solution.py:525
  102.2 17.5 %prefill_attention.1 = (bf16[17,128,512]{2,1,0:T(8,128)(2,1)}, f32[17,1,512]{2,1,0:T(1,128)}) custom-call(s32[8,4]{1,0:T(8,128)} %gather_fusion.3, s32[8,4]{1,0:T(8,128)} %gather_fusion.4, s32[8]{0:T(128)} %copy-done.4, s32[8]{0:T(128)} %get-tuple-element.35.local, bf16[528,2048]{1,0:T(8,128)(2,1)} %bitcast.40, ...), custom_call_target="tpu_custom_call" | custom-call | tf_op jit(solution)/shard_map/prefill_attention/pallas_call | solution.py:568
  119.7 10.2 %decode_attention.1 = (bf16[17,128,512]{2,1,0:T(8,128)(2,1)}, f32[17,1,512]{2,1,0:T(1,128)}) custom-call(s32[8,4]{1,0:T(8,128)} %gather_fusion, s32[8,4]{1,0:T(8,128)} %gather_fusion.1, s32[8]{0:T(128)} %get-tuple-element.20.home, s32[8]{0:T(128)} %get-tuple-element.19.local, s32[8]{0:T(128)} %copy-done.3, ...), custom_call_target="tpu_custom_call", output_to_operand_aliasing={{0}: (12, {}), {1}: (13, {})} | custom-call | tf_op jit(solution)/shard_map/decode_attention/pallas_call | solution.py:587
  129.9 64.5 %reduce_outputs.1 = (bf16[17,128,512]{2,1,0:T(8,128)(2,1)}, f32[17,1,512]{2,1,0:T(1,128)}) custom-call(bf16[17,128,512]{2,1,0:T(8,128)(2,1)} %get-tuple-element.12.o, f32[17,1,512]{2,1,0:T(1,128)} %get-tuple-element.13.e), custom_call_target="tpu_custom_call" | custom-call | tf_op jit(solution)/shard_map/reduce_outputs/pallas_call | solution.py:390
  194.4 3.5 %finish.1 = bf16[4,64,2048]{2,1,0:T(8,128)(2,1)} custom-call(s32[4]{0:T(128)} %maximum_reduce_fusion.slot, s32[4]{0:T(128)} %dynamic_slice.19.flag, s32[1]{0:T(128)} %bitcast.1.first, bf16[17,128,512]{2,1,0:T(8,128)(2,1)} %get-tuple-element.14.o_ref.od_ref, bf16[17,128,512]{2,1,0:T(8,128)(2,1)} %get-tuple-element.14.o_ref.od_ref), custom_call_target="tpu_custom_call" | custom-call | tf_op jit(solution)/shard_map/finish/pallas_call | solution.py:610
  197.9 9.8 %all-gather.2.cloned.1.call-done = bf16[4,64,4096]{2,1,0:T(8,128)(2,1)} async-done(((bf16[4,64,2048]{2,1,0:T(8,128)(2,1)}), bf16[4,64,4096]{2,1,0:T(8,128)(2,1)}) %all-gather.2.cloned.1.call-update) | async-done | bytes 2097168 | tf_op jit(solution)/shard_map/all_gather | solution.py:624
  207.8 3.1 %copy.33 = bf16[4,64,4096]{2,1,0:T(8,128)(2,1)} copy(bf16[4,64,4096]{2,1,0:T(8,128)(2,1)} %all-gather.2.cloned.1.call-done) | data formatting | bytes 4194304
  (38 shorter events, 0.7 us)
Async XLA Ops:
  6.5 13.1 %copy-start = (bf16[4,64,4096]{2,1,0:T(8,128)(2,1)S(1)}, bf16[4,64,4096]{2,1,0:T(8,128)(2,1)}, u32[]{:S(2)}) copy-start(bf16[4,64,4096]{2,1,0:T(8,128)(2,1)} %param.6) | copy-start | bytes 6291460
  6.5 201.2 %all-gather.2.cloned.1.call-start = ((), (), s32[]{:S(2)}) async-start(), calls=%async_computation | async-start | bytes 3145728 | tf_op jit(solution)/shard_map/all_gather | solution.py:624
  6.5 6.4 %copy-start.6 = (s32[16]{0:T(128)S(1)}, s32[16]{0:T(128)}, u32[]{:S(2)}) copy-start(s32[16]{0:T(128)} %param.11) | copy-start | bytes 196
  6.5 6.9 %copy-start.2 = (s32[16,16]{1,0:T(8,128)S(1)}, s32[16,16]{1,0:T(8,128)}, u32[]{:S(2)}) copy-start(s32[16,16]{1,0:T(8,128)} %param.9) | copy-start | bytes 3076
  6.5 7.1 %copy-start.5 = (s32[16]{0:T(128)S(1)}, s32[16]{0:T(128)}, u32[]{:S(2)}) copy-start(s32[16]{0:T(128)} %param.10) | copy-start | bytes 196
  12.4 84.4 %collective-permute-start = (bf16[21,2,128,256]{3,2,1,0:T(8,128)(2,1)}, bf16[21,2,128,256]{3,2,1,0:T(8,128)(2,1)}, u32[]{:S(2)}, u32[]{:S(2)}) collective-permute-start(bf16[21,2,128,256]{3,2,1,0:T(8,128)(2,1)} %get-tuple-element.24), channel_id=1, source_target_pairs={{0,1},{1,0},{2,3},{3,2},{4,5},{5,4},{6,7},{7,6},{8,9},{9,8},{10,11... | collective-permute-start | bytes 8257544 | tf_op jit(solution)/shard_map/ppermute | solution.py:524
  14.2 7.7 %copy-start.3 = (s32[8]{0:T(128)}, s32[8]{0:T(128)S(1)}, u32[]{:S(2)}) copy-start(s32[8]{0:T(128)S(1)} %select_reduce_fusion.3.seq) | copy-start | bytes 100
  19.5 2.4 %copy-start.4 = (s32[8]{0:T(128)}, s32[8]{0:T(128)S(1)}, u32[]{:S(2)}) copy-start(s32[8]{0:T(128)S(1)} %get-tuple-element.36.home) | copy-start | bytes 100
  25.3 70.1 %copy-start.1 = (bf16[4,64,2,512]{3,2,1,0:T(2,128)(2,1)S(1)}, bf16[4,64,2,512]{3,2,1,0:T(2,128)(2,1)}, u32[]{:S(2)}) copy-start(bf16[4,64,2,512]{3,2,1,0:T(2,128)(2,1)} %param.7) | copy-start | bytes 1572868
Sparse Core Ops, SparseCore 0:
  198.1 9.6 all-gather.1

commit v3 on v2

--- a/solution.py
+++ b/solution.py
@@ -415,9 +415,10 @@
 def partial_outputs(query, blocks):
     scored = [jnp.where(mask, scores_of(keys, query), NEG_FILL) for keys, _, mask in blocks]
     peak = functools.reduce(jnp.maximum, [jnp.max(s, axis=0, keepdims=True) for s in scored])
+    peak = jnp.maximum(peak, 0.1 * NEG_FILL)
     acc, total = None, None
-    for s, (_, values, mask) in zip(scored, blocks):
-        weights = jnp.where(mask, jnp.exp(s - peak), 0.0)
+    for s, (_, values, _) in zip(scored, blocks):
+        weights = jnp.exp(s - peak)
         part = jnp.sum(weights, axis=0, keepdims=True)
         prod = lax.dot_general(
             values, weights.astype(jnp.bfloat16), (((0,), (0,)), ((), ())), preferred_element_type=jnp.float32
@@ -512,7 +513,8 @@
     pages_dev, kv_width = kv_pages.shape[0], kv_pages.shape[3]
     seqs, page_count = page_table.shape
     owners = n * sub_count
-    most = sub_count * (page_count // owners)
+    each = page_count // owners
+    most = sub_count * each
     slots = seqs // 2
     group_size = query_width // kv_width
     part_width, query_part = kv_width // sub_count, query_width // sub_count
@@ -520,19 +522,21 @@
 
     other = (core + 1) % sub_count
     away = lax.dynamic_slice_in_dim(kv_pages, other * part_width, part_width, 3)
-    here = lax.dynamic_slice_in_dim(kv_pages, core * part_width, part_width, 3)
     came = lax.ppermute(away, "sub", [(c, (c + 1) % sub_count) for c in range(sub_count)])
-    pool = jnp.concatenate([here, came], axis=0)
 
     seq_ids = jnp.arange(seqs, dtype=jnp.int32)
-    owner = page_table // pages_dev
-    mine = (page_table >= 0) & (owner // sub_count == z)
-    index = page_table % pages_dev + jnp.where(owner % sub_count == core, 0, pages_dev)
-    rank = jnp.cumsum(mine.astype(jnp.int32), axis=1) - 1
-    picked = mine[:, :, None] & (rank[:, :, None] == jnp.arange(most, dtype=jnp.int32))
+    owner = jnp.where(page_table >= 0, page_table // pages_dev, -1)
+    sources = z * sub_count + jnp.stack([core, other])
+    mine = owner[None] == sources[:, None, None]
+    rank = jnp.cumsum(mine.astype(jnp.int32), axis=2) - 1
+    picked = mine[..., None] & (rank[..., None] == jnp.arange(each, dtype=jnp.int32))
     tokens = jnp.clip(cached_len[:, None] - PAGE * jnp.arange(page_count, dtype=jnp.int32), 0, PAGE)
-    page_rows = jnp.sum(jnp.where(picked, index[:, :, None], 0), axis=1)
-    valid_rows = jnp.sum(jnp.where(picked, tokens[:, :, None], 0), axis=1)
+
+    def listed(values):
+        found = jnp.sum(jnp.where(picked, values[None, :, :, None], 0), axis=2)
+        return jnp.moveaxis(found, 0, 1).reshape(seqs, most)
+
+    page_rows, valid_rows = listed(page_table % pages_dev), listed(tokens)
     flags = is_prefill == 1
     slot_of = jnp.cumsum(flags.astype(jnp.int32)) - 1
     place_of = jnp.cumsum((~flags).astype(jnp.int32)) - 1
@@ -543,11 +547,14 @@
 
     def tables(which):
         at_home = (which // seq_dev == z).astype(jnp.int32)
-        return page_rows[which], valid_rows[which], at_home, jnp.where(at_home == 1, which % seq_dev, 0)
+        places = jnp.where(at_home == 1, which % seq_dev, 0)
+        chosen = which[:, None, None] == seq_ids[None, :, None]
+        rows = [jnp.sum(jnp.where(chosen, x[None], 0), axis=1) for x in (page_rows, valid_rows)]
+        return rows[0], rows[1], at_home, jnp.append(places, core)
 
     slot_tables, rest_tables = tables(slot_seq), tables(rest_seq)
     my_queries = lax.dynamic_slice_in_dim(queries, core * query_part, query_part, 2)
-    own_slots = jnp.where((slot_tables[2] == 1)[:, None, None], my_queries[slot_tables[3]], 0)
+    own_slots = jnp.where((slot_tables[2] == 1)[:, None, None], my_queries[slot_tables[3][:slots]], 0)
     first_rows = jnp.where(
         (seq_ids // seq_dev == z)[:, None], jnp.tile(my_queries[:, 0], (n, 1)), 0
     )
@@ -560,7 +567,12 @@
     count = slots * heads + 1
 
     def page_spec(i):
-        return pl.BlockSpec((1, 2, PAGE, part_width), lambda j, pages, *_: (pages[j, i], 0, 0, 0))
+        if i >= each:
+            return pl.BlockSpec((1, 2, PAGE, part_width), lambda j, pages, *_: (pages[j, i], 0, 0, 0))
+        return pl.BlockSpec(
+            (1, 2, PAGE, part_width),
+            lambda j, pages, valid, home, local, *_: (pages[j, i], 0, 0, local[local.shape[0] - 1]),
+        )
 
     fresh_spec = pl.BlockSpec(
         (1, row_count, part_width), lambda j, pages, valid, home, local, *_: (local[j], 0, 0)
@@ -583,7 +595,7 @@
             jax.ShapeDtypeStruct((count, 1, lanes), jnp.float32),
         ],
         name="prefill_attention",
-    )(*slot_tables, gathered, *([pool] * most), fresh_keys, fresh_values)
+    )(*slot_tables, gathered, *([kv_pages] * each), *([came] * (most - each)), fresh_keys, fresh_values)
     o, e = pl.pallas_call(
         functools.partial(decode_kernel, most, heads, group_size, seqs),
         grid_spec=pltpu.PrefetchScalarGridSpec(
@@ -601,7 +613,7 @@
         out_shape=[jax.ShapeDtypeStruct(x.shape, x.dtype) for x in (o, e)],
         input_output_aliases={8 + most: 0, 9 + most: 1},
         name="decode_attention",
-    )(*rest_tables, rest_seq, gathered, *([pool] * most), fresh_keys, fresh_values, o, e)
+    )(*rest_tables, rest_seq, gathered, *([kv_pages] * each), *([came] * (most - each)), fresh_keys, fresh_values, o, e)
     o = reduce_outputs(o, e, n)
 
     first_seq = z * seq_dev
@@ -621,7 +633,11 @@
         out_shape=jax.ShapeDtypeStruct((seq_dev, row_count, query_part), jnp.bfloat16),
         name="finish",
     )(my_slots, my_flags, jnp.reshape(first_seq, (1,)).astype(jnp.int32), o, o)
-    return lax.all_gather(own_heads, "sub", axis=2, tiled=True)
+    pairs = [(c, (c + 1) % sub_count) for c in range(sub_count)]
+    came_heads = lax.ppermute(own_heads, "sub", pairs)
+    first_half = jnp.where(core == 0, own_heads, came_heads)
+    second_half = jnp.where(core == 0, came_heads, own_heads)
+    return jnp.concatenate([first_half, second_half], axis=2)
 
 
 def per_device(queries, new_kv, kv_pages, page_table, cached_len, is_prefill):

time: 218 us -> 189 us (0.87)
  between operations: 13.5 us -> 0.12 us
  local copies, waits for them, and re-layouts: 18.2 us -> 11 us
  waiting for transfers between devices: 9.84 us -> 2.87 us
    all_gather x1 -> x0, waiting for transfers between devices: 9.82 us -> none  [move_queries(): return lax.all_gather(own_heads, 'sub', axis=2, tiled=True)]
    gather x5 -> x1, local copies, waits for them, and re-layouts: 6.55 us -> 2 us  [move_queries(): my_queries[slot_tables[3][:slots]]]
    unnamed x16 -> x15, local copies, waits for them, and re-layouts: 3.17 us -> 0.04 us
    ppermute x0 -> x1, waiting for transfers between devices: none -> 2.87 us  [move_queries(): came_heads = lax.ppermute(own_heads, 'sub', pairs)]
    concatenate x1 -> x3, other arithmetic: 5.47 us -> 2.74 us  [the longest x1 1.54 us: move_queries(): return jnp.concatenate([first_half, second_half], axis=2)]
    reduce_sum x2 -> x4, local copies, waits for them, and re-layouts: 0.17 us -> 2.69 us  [tables(): jnp.sum(jnp.where(chosen, x[None], 0), axis=1)]
  transfers between devices with their start and end apart: 2 -> 2, of which waited for: 1 -> 1; matrix products, arithmetic and copies ran while one was open for 7% -> 8% of each run, Pallas kernels for 32% -> 37%
where the time goes in v3:
time: 189 us; the launch traced here: 188 us
  Pallas kernels  163 us (86%)
  local copies, waits for them, and re-layouts  11 us (6%)
  other arithmetic  10.6 us (6%)
  waiting for transfers between devices  2.87 us (2%)
    pallas_call x1, Pallas kernels, gather_queries(): pl.pallas_call(functools.partial(gather_queries_kernel, n, count), out_sh...  68.8 us
    pallas_call x1, Pallas kernels, reduce_outputs(): pl.pallas_call(functools.partial(reduce_outputs_kernel, n, count), out_sh...  64.7 us
    pallas_call x1, Pallas kernels, move_queries(): pl.pallas_call(functools.partial(prefill_kernel, most, heads, group_size)...  16.1 us
    pallas_call x1, Pallas kernels, move_queries(): pl.pallas_call(functools.partial(decode_kernel, most, heads, group_size,...  9.99 us
    dynamic_slice x1, local copies, waits for them, and re-layouts, move_queries(): away = lax.dynamic_slice_in_dim(kv_pages, other * part_width, part_width, 3)  3.8 us
  transfers between devices with their start and end apart: 2, of which 1 were waited for; matrix products, arithmetic and copies ran while one was open for 8% of the time, Pallas kernels for 37%

profile of v3, /device:TPU:0, one launch (start us, length us, event | category | flops | bytes accessed | tf_op | source)
XLA Modules:
  0.0 188.3 jit_solution(7964048683844832151)
XLA Ops:
  0.0 3.8 %constant_dynamic-slice_fusion.2 = bf16[21,2,128,256]{3,2,1,0:T(8,128)(2,1)} fusion(bf16[21,2,128,512]{3,2,1,0:T(8,128)(2,1)} %refs_1_.3, s32[]{:T(128)S(6)} %select_n.182), kind=kLoop, calls=%fused_computation.54 | loop fusion | bytes 5505028 | tf_op jit(solution)/shard_map/dynamic_slice | solution.py:524
  3.8 0.5 collective-permute-start
  4.4 0.1 fusion.8
  4.7 0.1 add_reduce_fusion
  4.8 0.1 select_reduce_fusion.6
  4.9 0.1 select_reduce_fusion.7.seq
  5.0 0.6 compare_select_fusion.2
  5.7 0.6 dynamic_slice.16.flag
  6.4 0.1 broadcast_in_dim.147
  6.7 0.3 reduce_window_sum.20
  7.1 0.2 select_reduce_fusion
  7.3 0.4 select_reduce_fusion.3
  7.7 0.7 copy.22.pages
  8.3 0.7 copy.24.pages
  9.0 0.7 copy.25.valid
  9.7 0.7 copy.23.valid
  10.6 2.0 %gather_fusion = bf16[8,64,2048]{2,1,0:T(8,128)(2,1)} fusion(bf16[4,64,2048]{2,1,0:T(8,128)(2,1)S(1)} %constant_dynamic-slice_fusion.3, s32[1024]{0:T(1024)S(1)} %pad_clamp_fusion), kind=kCustom, calls=%fused_computation | custom fusion | bytes 4194336 | tf_op jit(solution)/shard_map/gather | solution.py:557
  12.7 1.8 bitcast_select_fusion
  14.5 1.6 pad_maximum_fusion
  16.0 68.8 %gather_queries.1 = bf16[11,48,2048]{2,1,0:T(8,128)(2,1)} custom-call(bf16[11,48,2048]{2,1,0:T(8,128)(2,1)} %bitcast.43), custom_call_target="tpu_custom_call" | custom-call | tf_op jit(solution)/shard_map/gather_queries/pallas_call | solution.py:284
  84.9 0.7 maximum_reduce_fusion.slot
  85.6 0.6 pad_add_fusion.local
  86.2 0.6 pad_add_fusion.1.local
  86.8 0.6 constant_dynamic-slice_fusion.1
  87.4 0.7 copy_bitcast_fusion
  88.2 16.1 %prefill_attention.1 = (bf16[17,128,512]{2,1,0:T(8,128)(2,1)}, f32[17,1,512]{2,1,0:T(1,128)}) custom-call(s32[8,4]{1,0:T(8,128)} %copy.22.pages, s32[8,4]{1,0:T(8,128)} %copy.23.valid, s32[8]{0:T(128)} %copy-done.4, s32[9]{0:T(128)} %pad_add_fusion.1.local, bf16[528,2048]{1,0:T(8,128)(2,1)} %bitcast.41, bf16[21,2,128,512]{3,2,1,0:T(8,128)(2,1)} %refs_1_.3, ...), custom_call_target="tpu_custom_call" | custom-call | tf_op jit(solution)/shard_map/prefill_attention/pallas_call | solution.py:580
  104.3 10.0 %decode_attention.1 = (bf16[17,128,512]{2,1,0:T(8,128)(2,1)}, f32[17,1,512]{2,1,0:T(1,128)}) custom-call(s32[8,4]{1,0:T(8,128)} %copy.24.pages, s32[8,4]{1,0:T(8,128)} %copy.25.valid, s32[8]{0:T(128)} %get-tuple-element.26.home, s32[9]{0:T(128)} %pad_add_fusion.local, s32[8]{0:T(128)} %copy-done.3, ...), custom_call_target="tpu_custom_call", output_to_operand_aliasing={{0}: (12, {}), {1}: (13, {})} | custom-call | tf_op jit(solution)/shard_map/decode_attention/pallas_call | solution.py:599
  114.3 64.7 %reduce_outputs.1 = (bf16[17,128,512]{2,1,0:T(8,128)(2,1)}, f32[17,1,512]{2,1,0:T(1,128)}) custom-call(bf16[17,128,512]{2,1,0:T(8,128)(2,1)} %get-tuple-element.12.o, f32[17,1,512]{2,1,0:T(1,128)} %get-tuple-element.13.e), custom_call_target="tpu_custom_call" | custom-call | tf_op jit(solution)/shard_map/reduce_outputs/pallas_call | solution.py:390
  179.0 3.5 %finish.1 = bf16[4,64,2048]{2,1,0:T(8,128)(2,1)} custom-call(s32[4]{0:T(128)} %maximum_reduce_fusion.slot, s32[4]{0:T(128)} %dynamic_slice.16.flag, s32[1]{0:T(128)} %bitcast.1.first, bf16[17,128,512]{2,1,0:T(8,128)(2,1)} %get-tuple-element.14.o_ref.od_ref, bf16[17,128,512]{2,1,0:T(8,128)(2,1)} %get-tuple-element.14.o_ref.od_ref), custom_call_target="tpu_custom_call" | custom-call | tf_op jit(solution)/shard_map/finish/pallas_call | solution.py:622
  182.5 2.9 %collective-permute-done.1 = bf16[4,64,2048]{2,1,0:T(8,128)(2,1)S(1)} collective-permute-done((bf16[4,64,2048]{2,1,0:T(8,128)(2,1)}, bf16[4,64,2048]{2,1,0:T(8,128)(2,1)S(1)}, u32[]{:S(2)}, u32[]{:S(2)}) %collective-permute-start.1) | collective-permute-done | bytes 1048608 | tf_op jit(solution)/shard_map/ppermute | solution.py:637
  185.4 1.4 broadcast_select_fusion.1
  186.7 1.5 pad_maximum_fusion.1
  (38 shorter events, 0.9 us)
Async XLA Ops:
  0.0 10.4 %copy-start = (bf16[4,64,4096]{2,1,0:T(8,128)(2,1)S(1)}, bf16[4,64,4096]{2,1,0:T(8,128)(2,1)}, u32[]{:S(2)}) copy-start(bf16[4,64,4096]{2,1,0:T(8,128)(2,1)} %param.6) | copy-start | bytes 6291460
  0.0 4.3 %copy-start.6 = (s32[16]{0:T(128)S(1)}, s32[16]{0:T(128)}, u32[]{:S(2)}) copy-start(s32[16]{0:T(128)} %param.11) | copy-start | bytes 196
  0.0 6.6 %copy-start.2 = (s32[16,16]{1,0:T(8,128)S(1)}, s32[16,16]{1,0:T(8,128)}, u32[]{:S(2)}) copy-start(s32[16,16]{1,0:T(8,128)} %param.9) | copy-start | bytes 3076
  0.0 6.6 %copy-start.5 = (s32[16]{0:T(128)S(1)}, s32[16]{0:T(128)}, u32[]{:S(2)}) copy-start(s32[16]{0:T(128)} %param.10) | copy-start | bytes 196
  3.8 84.4 %collective-permute-start = (bf16[21,2,128,256]{3,2,1,0:T(8,128)(2,1)}, bf16[21,2,128,256]{3,2,1,0:T(8,128)(2,1)}, u32[]{:S(2)}, u32[]{:S(2)}) collective-permute-start(bf16[21,2,128,256]{3,2,1,0:T(8,128)(2,1)} %constant_dynamic-slice_fusion.2), channel_id=1, source_target_pairs={{0,1},{1,0},{2,3},{3,2},{4,5},{5,4},{6,7},{7,6},{8,9},{9,8},{10,11... | collective-permute-start | bytes 8257544 | tf_op jit(solution)/shard_map/ppermute | solution.py:525
  5.0 7.6 %copy-start.3 = (s32[8]{0:T(128)}, s32[8]{0:T(128)S(1)}, u32[]{:S(2)}) copy-start(s32[8]{0:T(128)S(1)} %select_reduce_fusion.7.seq) | copy-start | bytes 100
  5.6 7.0 %copy-start.4 = (s32[8]{0:T(128)}, s32[8]{0:T(128)S(1)}, u32[]{:S(2)}) copy-start(s32[8]{0:T(128)S(1)} %get-tuple-element.42.home) | copy-start | bytes 100
  16.0 70.8 %copy-start.1 = (bf16[4,64,2,512]{3,2,1,0:T(2,128)(2,1)S(1)}, bf16[4,64,2,512]{3,2,1,0:T(2,128)(2,1)}, u32[]{:S(2)}) copy-start(bf16[4,64,2,512]{3,2,1,0:T(2,128)(2,1)} %param.7) | copy-start | bytes 1572868
  182.5 2.9 %collective-permute-start.1 = (bf16[4,64,2048]{2,1,0:T(8,128)(2,1)}, bf16[4,64,2048]{2,1,0:T(8,128)(2,1)S(1)}, u32[]{:S(2)}, u32[]{:S(2)}) collective-permute-start(bf16[4,64,2048]{2,1,0:T(8,128)(2,1)} %finish.1), channel_id=1, source_target_pairs={{0,1},{1,0},{2,3},{3,2},{4,5},{5,4},{6,7},{7,6},{8,9},{9,8},{10,11... | collective-permute-start | bytes 3145736 | tf_op jit(solution)/shard_map/ppermute | solution.py:637

commit v4 on v3

--- a/solution.py
+++ b/solution.py
@@ -169,6 +169,7 @@
 
 MESH = pl.DeviceIdType.MESH
 SCALE = HD ** (-0.5)
+LOG2E = 1.4426950408889634
 
 
 def greet(z, n):
@@ -194,22 +195,22 @@
     )
 
 
-LAG = 2
-
-
-def line_steps(z, n, count, has_left, has_right, from_left, from_right, last):
+DEC_MAXP = 4
+
+
+def line_steps(z, n, count, lag, from_left, from_right, last):
     def guarded(c, work):
         @pl.when((c >= 0) & (c < count))
         def _():
             work(c)
 
     def step(s, carry):
-        guarded(s - LAG * z, from_left)
-        guarded(s - LAG * (n - 1 - z), from_right)
-        guarded(s - LAG * jnp.maximum(z, n - 1 - z), last)
+        guarded(s - lag * z, from_left)
+        guarded(s - lag * (n - 1 - z), from_right)
+        guarded(s - lag * jnp.maximum(z, n - 1 - z), last)
         return carry
 
-    lax.fori_loop(0, count + LAG * (n - 1), step, 0)
+    lax.fori_loop(0, count + lag * (n - 1), step, 0)
 
 
 def gather_queries_kernel(n, count, own, out, rin, rout, lin, lout, rs, rr, ls, lr):
@@ -259,7 +260,7 @@
         def _():
             out[c] = rout[c]
 
-    line_steps(z, n, count, has_left, has_right, from_left, from_right, last)
+    line_steps(z, n, count, 4, from_left, from_right, last)
 
     def drain(c, carry):
         @pl.when(has_right)
@@ -277,7 +278,7 @@
 
 def gather_queries(own, n):
     total, width = own.shape
-    rows = 48 if total % 48 == 0 else 16
+    rows = 16
     count = total // rows
     shape = (count, rows, width)
     buffer = pltpu.VMEM(shape, own.dtype)
@@ -367,7 +368,7 @@
             out[c] = ro[c]
             oute[c] = reo[c]
 
-    line_steps(z, n, count, has_left, has_right, from_left, from_right, last)
+    line_steps(z, n, count, 2, from_left, from_right, last)
 
     def drain(c, carry):
         @pl.when(has_right)
@@ -407,9 +408,7 @@
 
 
 def scores_of(keys, query):
-    return (
-        lax.dot_general(keys, query, (((1,), (1,)), ((), ())), preferred_element_type=jnp.float32) * SCALE
-    )
+    return lax.dot_general(keys, query, (((1,), (1,)), ((), ())), preferred_element_type=jnp.float32)
 
 
 def partial_outputs(query, blocks):
@@ -418,7 +417,7 @@
     peak = jnp.maximum(peak, 0.1 * NEG_FILL)
     acc, total = None, None
     for s, (_, values, _) in zip(scored, blocks):
-        weights = jnp.exp(s - peak)
+        weights = jnp.exp2((s - peak) * (SCALE * LOG2E))
         part = jnp.sum(weights, axis=0, keepdims=True)
         prod = lax.dot_general(
             values, weights.astype(jnp.bfloat16), (((0,), (0,)), ((), ())), preferred_element_type=jnp.float32
@@ -427,7 +426,7 @@
         total = part if total is None else total + part
     empty = total == 0.0
     total = jnp.where(empty, 1.0, total)
-    return acc * (1.0 / total), jnp.where(empty, NEG_FILL, peak + jnp.log(total))
+    return acc * (1.0 / total), jnp.where(empty, NEG_FILL, peak * SCALE + jnp.log(total))
 
 
 def prefill_kernel(most, heads, group_size, pages, valid, home, local, q_ref, *refs):
@@ -451,8 +450,8 @@
         e_ref[k] = e
 
 
-def decode_kernel(most, heads, group_size, seqs, pages, valid, home, local, seq, q_ref, *refs):
-    page_refs, (fk_ref, fv_ref, _, _, o_ref, e_ref) = refs[:most], refs[most:]
+def decode_kernel(columns, heads, group_size, seqs, pages, valid, home, local, seq, q_ref, *refs):
+    page_refs, (fk_ref, fv_ref, _, _, o_ref, e_ref) = refs[: len(columns)], refs[len(columns) :]
     j = pl.program_id(0)
     lanes = group_size * seqs
     fresh_rows = 16
@@ -469,7 +468,7 @@
         cols = slice(k * HD, (k + 1) * HD)
         query = stacked_heads(q_ref, k, group_size)
         blocks = [
-            (ref[0, 0, :, cols], ref[0, 1, :, cols], key_id < valid[j, i]) for i, ref in enumerate(page_refs)
+            (ref[0, 0, :, cols], ref[0, 1, :, cols], key_id < valid[j, i]) for i, ref in zip(columns, page_refs)
         ]
         fresh_mask = fresh_id < home[j]
         blocks.append((fk_ref[0, :fresh_rows, cols], fv_ref[0, :fresh_rows, cols], fresh_mask))
@@ -596,13 +595,15 @@
         ],
         name="prefill_attention",
     )(*slot_tables, gathered, *([kv_pages] * each), *([came] * (most - each)), fresh_keys, fresh_values)
+    few = min(each, -(-DEC_MAXP // owners))
+    columns = [*range(few), *range(each, each + few)]
     o, e = pl.pallas_call(
-        functools.partial(decode_kernel, most, heads, group_size, seqs),
+        functools.partial(decode_kernel, columns, heads, group_size, seqs),
         grid_spec=pltpu.PrefetchScalarGridSpec(
             num_scalar_prefetch=5,
             grid=(seqs - slots,),
             in_specs=[pl.BlockSpec((seqs, query_part), lambda j, *_: (slots * row_count // seqs, 0))]
-            + [page_spec(i) for i in range(most)]
+            + [page_spec(i) for i in columns]
             + [fresh_spec] * 2
             + [pl.BlockSpec(memory_space=pl.ANY)] * 2,
             out_specs=[
@@ -611,9 +612,9 @@
             ],
         ),
         out_shape=[jax.ShapeDtypeStruct(x.shape, x.dtype) for x in (o, e)],
-        input_output_aliases={8 + most: 0, 9 + most: 1},
+        input_output_aliases={8 + len(columns): 0, 9 + len(columns): 1},
         name="decode_attention",
-    )(*rest_tables, rest_seq, gathered, *([kv_pages] * each), *([came] * (most - each)), fresh_keys, fresh_values, o, e)
+    )(*rest_tables, rest_seq, gathered, *([kv_pages] * few), *([came] * few), fresh_keys, fresh_values, o, e)
     o = reduce_outputs(o, e, n)
 
     first_seq = z * seq_dev

time: 189 us -> 184 us (0.974)
  Pallas kernels: 163 us -> 159 us
    pallas_call x1, Pallas kernels: 68.8 us -> 64.8 us  [gather_queries(): pl.pallas_call(functools.partial(gather_queries_kernel, n, count), out_sh...]
  transfers between devices with their start and end apart: 2 -> 2, of which waited for: 1 -> 1; matrix products, arithmetic and copies ran while one was open for 8% -> 8% of each run, Pallas kernels for 37% -> 35%
where the time goes in v4:
time: 184 us
  Pallas kernels  159 us (86%)
  local copies, waits for them, and re-layouts  11 us (6%)
  other arithmetic  10.6 us (6%)
  waiting for transfers between devices  2.87 us (2%)
    pallas_call x1, Pallas kernels, reduce_outputs(): pl.pallas_call(functools.partial(reduce_outputs_kernel, n, count), out_sh...  65.1 us
    pallas_call x1, Pallas kernels, gather_queries(): pl.pallas_call(functools.partial(gather_queries_kernel, n, count), out_sh...  64.8 us
    pallas_call x1, Pallas kernels, move_queries(): pl.pallas_call(functools.partial(prefill_kernel, most, heads, group_size)...  15.8 us
    pallas_call x1, Pallas kernels, move_queries(): pl.pallas_call(functools.partial(decode_kernel, columns, heads, group_siz...  8.81 us
    pallas_call x1, Pallas kernels, move_queries(): pl.pallas_call(functools.partial(finish_kernel, heads, group_size, seqs),...  4.34 us
    dynamic_slice x1, local copies, waits for them, and re-layouts, move_queries(): away = lax.dynamic_slice_in_dim(kv_pages, other * part_width, part_width, 3)  3.8 us
  transfers between devices with their start and end apart: 2, of which 1 were waited for; matrix products, arithmetic and copies ran while one was open for 8% of the time, Pallas kernels for 35%

profile of v4, /device:TPU:0, one launch (start us, length us, event | category | flops | bytes accessed | tf_op | source)
XLA Modules:
  0.0 183.9 jit_solution(4184237534698645720)
XLA Ops:
  0.0 3.8 %constant_dynamic-slice_fusion.2 = bf16[21,2,128,256]{3,2,1,0:T(8,128)(2,1)} fusion(bf16[21,2,128,512]{3,2,1,0:T(8,128)(2,1)} %refs_0_.3, s32[]{:T(128)S(6)} %select_n.182), kind=kLoop, calls=%fused_computation.54 | loop fusion | bytes 5505028 | tf_op jit(solution)/shard_map/dynamic_slice | solution.py:523
  3.8 0.5 collective-permute-start
  4.4 0.1 fusion.8
  4.7 0.1 add_reduce_fusion
  4.8 0.1 select_reduce_fusion.6
  4.9 0.1 select_reduce_fusion.7.seq
  5.0 0.6 compare_select_fusion.2
  5.7 0.6 dynamic_slice.16.flag
  6.4 0.1 broadcast_in_dim.147
  6.7 0.3 reduce_window_sum.20
  7.1 0.2 select_reduce_fusion
  7.3 0.4 select_reduce_fusion.3
  7.7 0.7 copy.22.pages
  8.3 0.7 copy.24.pages
  9.0 0.7 copy.25.valid
  9.7 0.7 copy.23.valid
  10.6 2.0 %gather_fusion = bf16[8,64,2048]{2,1,0:T(8,128)(2,1)} fusion(bf16[4,64,2048]{2,1,0:T(8,128)(2,1)S(1)} %constant_dynamic-slice_fusion.3, s32[1024]{0:T(1024)S(1)} %pad_clamp_fusion), kind=kCustom, calls=%fused_computation | custom fusion | bytes 4194336 | tf_op jit(solution)/shard_map/gather | solution.py:556
  12.7 1.8 bitcast_select_fusion
  14.5 1.6 pad_maximum_fusion
  16.0 64.8 %gather_queries.1 = bf16[33,16,2048]{2,1,0:T(8,128)(2,1)} custom-call(bf16[33,16,2048]{2,1,0:T(8,128)(2,1)} %bitcast.43), custom_call_target="tpu_custom_call" | custom-call | tf_op jit(solution)/shard_map/gather_queries/pallas_call | solution.py:285
  80.8 0.7 maximum_reduce_fusion.slot
  81.5 0.6 pad_add_fusion.local
  82.1 0.6 pad_add_fusion.1.local
  82.7 0.6 constant_dynamic-slice_fusion.1
  83.4 0.7 copy_bitcast_fusion
  84.1 15.8 %prefill_attention.1 = (bf16[17,128,512]{2,1,0:T(8,128)(2,1)}, f32[17,1,512]{2,1,0:T(1,128)}) custom-call(s32[8,4]{1,0:T(8,128)} %copy.22.pages, s32[8,4]{1,0:T(8,128)} %copy.23.valid, s32[8]{0:T(128)} %copy-done.4, s32[9]{0:T(128)} %pad_add_fusion.1.local, bf16[528,2048]{1,0:T(8,128)(2,1)} %bitcast.41, bf16[21,2,128,512]{3,2,1,0:T(8,128)(2,1)} %refs_0_.3, ...), custom_call_target="tpu_custom_call" | custom-call | tf_op jit(solution)/shard_map/prefill_attention/pallas_call | solution.py:579
  99.9 8.8 %decode_attention.1 = (bf16[17,128,512]{2,1,0:T(8,128)(2,1)}, f32[17,1,512]{2,1,0:T(1,128)}) custom-call(s32[8,4]{1,0:T(8,128)} %copy.24.pages, s32[8,4]{1,0:T(8,128)} %copy.25.valid, s32[8]{0:T(128)} %get-tuple-element.26.home, s32[9]{0:T(128)} %pad_add_fusion.local, s32[8]{0:T(128)} %copy-done.3, ...), custom_call_target="tpu_custom_call", output_to_operand_aliasing={{0}: (10, {}), {1}: (11, {})} | custom-call | tf_op jit(solution)/shard_map/decode_attention/pallas_call | solution.py:600
  108.7 65.1 %reduce_outputs.1 = (bf16[17,128,512]{2,1,0:T(8,128)(2,1)}, f32[17,1,512]{2,1,0:T(1,128)}) custom-call(bf16[17,128,512]{2,1,0:T(8,128)(2,1)} %get-tuple-element.12.o, f32[17,1,512]{2,1,0:T(1,128)} %get-tuple-element.13.e), custom_call_target="tpu_custom_call" | custom-call | tf_op jit(solution)/shard_map/reduce_outputs/pallas_call | solution.py:391
  173.8 4.3 %finish.1 = bf16[4,64,2048]{2,1,0:T(8,128)(2,1)} custom-call(s32[4]{0:T(128)} %maximum_reduce_fusion.slot, s32[4]{0:T(128)} %dynamic_slice.16.flag, s32[1]{0:T(128)} %bitcast.1.first, bf16[17,128,512]{2,1,0:T(8,128)(2,1)} %get-tuple-element.14.o_ref.od_ref, bf16[17,128,512]{2,1,0:T(8,128)(2,1)} %get-tuple-element.14.o_ref.od_ref), custom_call_target="tpu_custom_call" | custom-call | tf_op jit(solution)/shard_map/finish/pallas_call | solution.py:623
  178.1 2.9 %collective-permute-done.1 = bf16[4,64,2048]{2,1,0:T(8,128)(2,1)S(1)} collective-permute-done((bf16[4,64,2048]{2,1,0:T(8,128)(2,1)}, bf16[4,64,2048]{2,1,0:T(8,128)(2,1)S(1)}, u32[]{:S(2)}, u32[]{:S(2)}) %collective-permute-start.1) | collective-permute-done | bytes 1048608 | tf_op jit(solution)/shard_map/ppermute | solution.py:638
  181.0 1.4 broadcast_select_fusion.1
  182.3 1.5 pad_maximum_fusion.1
  (38 shorter events, 0.9 us)
Async XLA Ops:
  0.0 10.4 %copy-start = (bf16[4,64,4096]{2,1,0:T(8,128)(2,1)S(1)}, bf16[4,64,4096]{2,1,0:T(8,128)(2,1)}, u32[]{:S(2)}) copy-start(bf16[4,64,4096]{2,1,0:T(8,128)(2,1)} %param.6) | copy-start | bytes 6291460
  0.0 4.3 %copy-start.6 = (s32[16]{0:T(128)S(1)}, s32[16]{0:T(128)}, u32[]{:S(2)}) copy-start(s32[16]{0:T(128)} %param.11) | copy-start | bytes 196
  0.0 6.6 %copy-start.2 = (s32[16,16]{1,0:T(8,128)S(1)}, s32[16,16]{1,0:T(8,128)}, u32[]{:S(2)}) copy-start(s32[16,16]{1,0:T(8,128)} %param.9) | copy-start | bytes 3076
  0.0 6.6 %copy-start.5 = (s32[16]{0:T(128)S(1)}, s32[16]{0:T(128)}, u32[]{:S(2)}) copy-start(s32[16]{0:T(128)} %param.10) | copy-start | bytes 196
  3.8 80.3 %collective-permute-start = (bf16[21,2,128,256]{3,2,1,0:T(8,128)(2,1)}, bf16[21,2,128,256]{3,2,1,0:T(8,128)(2,1)}, u32[]{:S(2)}, u32[]{:S(2)}) collective-permute-start(bf16[21,2,128,256]{3,2,1,0:T(8,128)(2,1)} %constant_dynamic-slice_fusion.2), channel_id=1, source_target_pairs={{0,1},{1,0},{2,3},{3,2},{4,5},{5,4},{6,7},{7,6},{8,9},{9,8},{10,11... | collective-permute-start | bytes 8257544 | tf_op jit(solution)/shard_map/ppermute | solution.py:524
  5.0 7.6 %copy-start.3 = (s32[8]{0:T(128)}, s32[8]{0:T(128)S(1)}, u32[]{:S(2)}) copy-start(s32[8]{0:T(128)S(1)} %select_reduce_fusion.7.seq) | copy-start | bytes 100
  5.6 7.0 %copy-start.4 = (s32[8]{0:T(128)}, s32[8]{0:T(128)S(1)}, u32[]{:S(2)}) copy-start(s32[8]{0:T(128)S(1)} %get-tuple-element.42.home) | copy-start | bytes 100
  16.0 66.7 %copy-start.1 = (bf16[4,64,2,512]{3,2,1,0:T(2,128)(2,1)S(1)}, bf16[4,64,2,512]{3,2,1,0:T(2,128)(2,1)}, u32[]{:S(2)}) copy-start(bf16[4,64,2,512]{3,2,1,0:T(2,128)(2,1)} %param.7) | copy-start | bytes 1572868
  178.1 2.9 %collective-permute-start.1 = (bf16[4,64,2048]{2,1,0:T(8,128)(2,1)}, bf16[4,64,2048]{2,1,0:T(8,128)(2,1)S(1)}, u32[]{:S(2)}, u32[]{:S(2)}) collective-permute-start(bf16[4,64,2048]{2,1,0:T(8,128)(2,1)} %finish.1), channel_id=1, source_target_pairs={{0,1},{1,0},{2,3},{3,2},{4,5},{5,4},{6,7},{7,6},{8,9},{9,8},{10,11... | collective-permute-start | bytes 3145736 | tf_op jit(solution)/shard_map/ppermute | solution.py:638
